TPU v7x, 32 devices: a whole 2x2x4 slice. The times are simulated.
32 devices in a mesh: pts: 16 (over z, x, core), cen: 2 (over y).
Axes of the slice: x: 2, y: 2, z: 4, core: 2. Of those that a mesh axis runs over, the one named last changes fastest.
Arguments:
- states: bfloat16 [8192, 512], P(('pts', 'cen')), may hold values from -48 to 48
- first_weight: bfloat16 [512, 1024], replicated, may hold values from -0.25 to 0.25
- first_bias: float32 [1024], replicated, may hold values from -4 to 4
- second_weight: bfloat16 [1024, 256], replicated, may hold values from -0.1875 to 0.1875
- centroids: bfloat16 [2, 4096, 256], P('cen'), may hold values from -3.59375 to 3.59375
Outputs:
- new_centroids: float32 [2, 4096, 256], P('cen', 'pts')
- sample_blended_penalty: float32 [8192], P(('pts', 'cen'))
All inputs are finite; a program needn't handle non-finite values.
Results may differ from a plain program's by a relative error of at most 0.0061.
Values may be sent and summed in bfloat16 or wider, within the bound.
A program may use at most 128 MiB of HBM per device.

v0:
```python
import functools

import jax
import jax.numpy as jnp
from jax import lax
from jax.experimental import pallas as pl
from jax.experimental.pallas import tpu as pltpu
from jax.sharding import PartitionSpec as P

smoothing_scale = 16.0
MESH = pl.DeviceIdType.MESH
NT = (((1,), (1,)), ((), ()))


def scaled_squares(rows):
    wide = rows.astype(jnp.float32)
    return jnp.sum(wide * wide, axis=1, keepdims=True) / smoothing_scale


def kernel(
    n_pts, n_cen, states_hbm, first_hbm, bias_ref, second_hbm, cen_hbm, out_ref, pen_ref,
    states_ref, first_ref, second_ref, cen_ref, load_sem,
    allc, stat, norm, weighted, counts, own_sq,
    recv, half, stat_recv, norm_recv,
    send_up, send_down, send_x, send_c, send_core, send_hx, send_hc, send_stat, send_norm, own_sem,
):
    n, width = states_ref.shape[0], second_ref.shape[1]
    loads = [
        pltpu.make_async_copy(src, dst, load_sem.at[i])
        for i, (src, dst) in enumerate(
            (
                (states_hbm, states_ref),
                (first_hbm, first_ref),
                (second_hbm, second_ref),
                (cen_hbm.at[0], cen_ref),
            )
        )
    ]
    for load in loads:
        load.start()
    n_z = n_pts // 4
    p, c = lax.axis_index("pts"), lax.axis_index("cen")
    core, x, z = lax.rem(p, 2), lax.rem(p // 2, 2), p // 4

    def pts_of(zi, xi, ki):
        return (zi * 2 + xi) * 2 + ki

    def z_at(k):
        return lax.rem(z + k, n_z)

    def c_at(j):
        return lax.rem(c + j, n_cen)

    def block(zi, xi, ki, ci):
        return pts_of(zi, xi, ki) * n_cen + ci

    x_peer = (pts_of(z, 1 - x, core), c)
    core_peer = (pts_of(z, x, 1 - core), c)
    mine = block(z, x, core, c)

    def remote(src, dst, send_sem, recv_sem, peer):
        return pltpu.make_async_remote_copy(
            src_ref=src, dst_ref=dst, send_sem=send_sem, recv_sem=recv_sem,
            device_id=peer, device_id_type=MESH,
        )

    def push(copy):
        copy.start()

    def whole(b, send_sem, peer):
        push(remote(allc.at[b], allc.at[b], send_sem, recv.at[b], peer))

    def part(b, h, send_sem, peer):
        rows = pl.ds(h * (n // 2), n // 2)
        push(remote(allc.at[b, rows], allc.at[b, rows], send_sem, half.at[b, h], peer))

    def arrived(b):
        remote(allc.at[b], allc.at[b], own_sem, recv.at[b], core_peer).wait_recv()

    def part_arrived(b, h):
        rows = pl.ds(h * (n // 2), n // 2)
        remote(allc.at[b, rows], allc.at[b, rows], own_sem, half.at[b, h], core_peer).wait_recv()

    has_up, has_down = z < n_z - 1, z > 0
    up_peer = (pts_of(lax.rem(z + 1, n_z), x, core), c)
    down_peer = (pts_of(lax.rem(z + n_z - 1, n_z), x, core), c)

    def at_distance(d, visit):
        if d == 0:
            visit(z)
            return

        @pl.when(z + d < n_z)
        def _():
            visit(z + d)

        @pl.when(z >= d)
        def _():
            visit(z - d)

    def fan_out(zi):
        b = block(zi, x, core, c)

        @pl.when(jnp.logical_and(has_up, zi <= z))
        def _():
            whole(b, send_up.at[zi], up_peer)

        @pl.when(jnp.logical_and(has_down, zi >= z))
        def _():
            whole(b, send_down.at[zi], down_peer)

        for j in range(1, n_cen):
            whole(b, send_c.at[zi, j], (p, c_at(j)))
        whole(b, send_x.at[zi], x_peer)
        whole(b, send_core.at[zi, 0, 0], core_peer)

    def from_line(zi):
        arrived(block(zi, x, core, c))
        fan_out(zi)

    def from_cen(zi):
        for j in range(1, n_cen):
            b = block(zi, x, core, c_at(j))
            arrived(b)
            part(b, 1, send_hx.at[zi, j], x_peer)
            whole(b, send_core.at[zi, 0, j], core_peer)

    def from_x(zi):
        b = block(zi, 1 - x, core, c)
        arrived(b)
        for j in range(1, n_cen):
            part(b, 0, send_hc.at[zi, j], (p, c_at(j)))
        whole(b, send_core.at[zi, 1, 0], core_peer)

    def from_both(zi):
        for j in range(1, n_cen):
            b = block(zi, 1 - x, core, c_at(j))
            part_arrived(b, 0)
            part_arrived(b, 1)
            whole(b, send_core.at[zi, 1, j], core_peer)

    barrier = pltpu.get_barrier_semaphore()
    for k in range(1, n_pts):
        pl.semaphore_signal(
            barrier, inc=1, device_id=(lax.rem(p + k, n_pts), c), device_id_type=MESH
        )
    for j in range(1, n_cen):
        pl.semaphore_signal(barrier, inc=1, device_id=(p, c_at(j)), device_id_type=MESH)
    loads[0].wait()
    loads[1].wait()
    pre = jnp.dot(states_ref[...], first_ref[...], preferred_element_type=jnp.float32)
    hidden = jax.nn.gelu(pre + bias_ref[...][None, :]).astype(jnp.bfloat16)
    loads[2].wait()
    allc[mine] = jnp.dot(
        hidden, second_ref[...], preferred_element_type=jnp.float32
    ).astype(jnp.bfloat16)
    loads[3].wait()
    owned = out_ref.shape[0]
    own_rows = pl.ds(pl.multiple_of(p * owned, owned), owned)
    own_sq[...] = scaled_squares(cen_ref[own_rows, :])
    pl.semaphore_wait(barrier, n_pts - 1 + n_cen - 1)
    fan_out(z)

    from_cen(z)

    tile = min(512, cen_ref.shape[0])
    group_rows = n * n_cen
    group = pl.ds(p * n_cen, n_cen)

    def stats_step(i, carry):
        peak, total = carry
        centers = cen_ref[pl.ds(pl.multiple_of(i * tile, tile), tile), :]
        rows = allc[group].reshape(group_rows, width)
        scores = lax.dot_general(centers, rows, NT, preferred_element_type=jnp.float32)
        scores = scores * (2.0 / smoothing_scale) - scaled_squares(centers)
        peak_next = jnp.maximum(peak, jnp.max(scores, axis=0, keepdims=True))
        total_next = total * jnp.exp(peak - peak_next) + jnp.sum(
            jnp.exp(scores - peak_next), axis=0, keepdims=True
        )
        return peak_next, total_next

    tiles = cen_ref.shape[0] // tile
    stats = (
        jnp.full((1, group_rows), -jnp.inf, jnp.float32),
        jnp.zeros((1, group_rows), jnp.float32),
    )
    for d in range(1, n_z + 1):
        lo, hi = tiles * (d - 1) // n_z, tiles * d // n_z
        stats = lax.fori_loop(lo, hi, stats_step, stats)
        if d < n_z:
            at_distance(d, from_line)
            at_distance(d - 1, from_x)
            if d > 1:
                at_distance(d - 1, from_cen)
    peak, total = stats
    first = lax.broadcasted_iota(jnp.int32, (8, n), 0) == 0
    for j in range(n_cen):
        cols = slice(j * n, (j + 1) * n)
        stat[c, j] = jnp.where(first, peak[:, cols], total[:, cols])
    for j in range(1, n_cen):
        push(remote(stat.at[c], stat.at[c], send_stat.at[j], stat_recv.at[c], (p, c_at(j))))
    at_distance(n_z - 1, from_x)
    if n_z > 1:
        at_distance(n_z - 1, from_cen)

    for j in range(1, n_cen):
        s = c_at(j)
        remote(stat.at[s], stat.at[s], own_sem, stat_recv.at[s], (p, s)).wait_recv()
    for j in range(n_cen):
        top = stat[0, j][0:1, :]
        for s in range(1, n_cen):
            top = jnp.maximum(top, stat[s, j][0:1, :])
        mass = jnp.zeros_like(top)
        for s in range(n_cen):
            piece = stat[s, j]
            mass = mass + piece[1:2, :] * jnp.exp(piece[0:1, :] - top)
        norm[p, :, j * n:(j + 1) * n] = jnp.broadcast_to(top + jnp.log(mass), (8, n))
    for k in range(1, n_pts):
        push(
            remote(
                norm.at[p], norm.at[p], send_norm.at[k], norm_recv.at[p],
                (lax.rem(p + k, n_pts), c),
            )
        )
    wide = allc[mine].astype(jnp.float32)
    lengths = lax.dot_general(
        jnp.ones((8, width), jnp.float32), wide * wide, NT,
        preferred_element_type=jnp.float32, precision=lax.Precision.HIGHEST,
    )
    pen_ref[...] = (-(smoothing_scale / width)) * (
        norm[p, 0:1, pl.ds(pl.multiple_of(c * n, n), n)] - lengths[0:1, :] / smoothing_scale
    )

    for k in range(1, n_pts):
        s = lax.rem(p + k, n_pts)
        remote(norm.at[s], norm.at[s], own_sem, norm_recv.at[s], (s, c)).wait_recv()

    weighted[...] = jnp.zeros_like(weighted)
    counts[...] = jnp.zeros_like(counts)

    def consume(pi):
        rows = allc[pl.ds(pi * n_cen, n_cen)].reshape(group_rows, width)
        scores = lax.dot_general(
            cen_ref[own_rows, :], rows, NT, preferred_element_type=jnp.float32
        )
        resp = jnp.exp(scores * (2.0 / smoothing_scale) - own_sq[...] - norm[pi, 0:1, :])
        lanes = resp[:, 0:128]
        for q in range(1, group_rows // 128):
            lanes = lanes + resp[:, q * 128:(q + 1) * 128]
        counts[...] += lanes
        weighted[...] += jnp.dot(
            resp.astype(jnp.bfloat16), rows, preferred_element_type=jnp.float32
        )

    def line(i, _):
        from_both(z_at(i))
        consume(pts_of(z_at(i), x, core))
        return 0

    def across(i, _):
        consume(pts_of(z_at(i), 1 - x, core))
        return 0

    def other_core(i, _):
        zi, xi = z_at(lax.rem(i, n_z)), lax.rem(x + i // n_z, 2)
        for ci in range(n_cen):
            arrived(block(zi, xi, 1 - core, ci))
        consume(pts_of(zi, xi, 1 - core))
        return 0

    lax.fori_loop(0, n_z, line, 0, unroll=n_z <= 4)
    lax.fori_loop(0, n_z, across, 0, unroll=n_z <= 4)
    lax.fori_loop(0, 2 * n_z, other_core, 0, unroll=n_z <= 4)

    tally = jnp.sum(counts[...], axis=1, keepdims=True)
    out_ref[...] = (weighted[...] + cen_ref[own_rows, :].astype(jnp.float32)) / (tally + 1.0)

    def left(ref, send_sem):
        remote(ref, ref, send_sem, own_sem, core_peer).wait_send()

    block_ref, half_ref = allc.at[0], allc.at[0, pl.ds(0, n // 2)]
    for zi in range(n_z):

        @pl.when(jnp.logical_and(has_up, zi <= z))
        def _():
            left(block_ref, send_up.at[zi])

        @pl.when(jnp.logical_and(has_down, zi >= z))
        def _():
            left(block_ref, send_down.at[zi])

        left(block_ref, send_x.at[zi])
        for j in range(n_cen):
            left(block_ref, send_core.at[zi, 0, j])
            left(block_ref, send_core.at[zi, 1, j])
            if j > 0:
                left(block_ref, send_c.at[zi, j])
                left(half_ref, send_hx.at[zi, j])
                left(half_ref, send_hc.at[zi, j])
    for j in range(1, n_cen):
        left(stat.at[0], send_stat.at[j])
    for k in range(1, n_pts):
        left(norm.at[0], send_norm.at[k])


def finish(fresh_ref, pen_ref, out_ref, cost_ref):
    out_ref[0] = fresh_ref[...]
    cost_ref[...] = pen_ref[0]


def body(n_pts, n_cen, states, first_weight, first_bias, second_weight, centroids):
    n, width = states.shape[0], second_weight.shape[1]
    owned = centroids.shape[1] // n_pts
    n_z = n_pts // 4
    dma = pltpu.SemaphoreType.DMA
    fresh, penalty = pl.pallas_call(
        functools.partial(kernel, n_pts, n_cen),
        out_shape=(
            jax.ShapeDtypeStruct((owned, width), jnp.float32),
            jax.ShapeDtypeStruct((1, n), jnp.float32),
        ),
        in_specs=[
            pl.BlockSpec(memory_space=pl.ANY),
            pl.BlockSpec(memory_space=pl.ANY),
            pl.BlockSpec(memory_space=pltpu.VMEM),
            pl.BlockSpec(memory_space=pl.ANY),
            pl.BlockSpec(memory_space=pl.ANY),
        ],
        out_specs=(pl.BlockSpec(memory_space=pltpu.VMEM),) * 2,
        scratch_shapes=[
            pltpu.VMEM(states.shape, states.dtype),
            pltpu.VMEM(first_weight.shape, first_weight.dtype),
            pltpu.VMEM(second_weight.shape, second_weight.dtype),
            pltpu.VMEM(centroids.shape[1:], centroids.dtype),
            dma((4,)),
            pltpu.VMEM((n_pts * n_cen, n, width), jnp.bfloat16),
            pltpu.VMEM((n_cen, n_cen, 8, n), jnp.float32),
            pltpu.VMEM((n_pts, 8, n_cen * n), jnp.float32),
            pltpu.VMEM((owned, width), jnp.float32),
            pltpu.VMEM((owned, 128), jnp.float32),
            pltpu.VMEM((owned, 1), jnp.float32),
            dma((n_pts * n_cen,)),
            dma((n_pts * n_cen, 2)),
            dma((n_cen,)),
            dma((n_pts,)),
            dma((n_z,)),
            dma((n_z,)),
            dma((n_z,)),
            dma((n_z, n_cen)),
            dma((n_z, 2, n_cen)),
            dma((n_z, n_cen)),
            dma((n_z, n_cen)),
            dma((n_cen,)),
            dma((n_pts,)),
            dma,
        ],
        compiler_params=pltpu.CompilerParams(
            collective_id=0, has_side_effects=True, vmem_limit_bytes=60 * 1024 * 1024
        ),
    )(states, first_weight, first_bias, second_weight, centroids)
    return pl.pallas_call(
        finish,
        out_shape=(
            jax.ShapeDtypeStruct((1, owned, width), jnp.float32),
            jax.ShapeDtypeStruct((n,), jnp.float32),
        ),
        in_specs=[pl.BlockSpec(memory_space=pltpu.VMEM)] * 2,
        out_specs=(pl.BlockSpec(memory_space=pltpu.VMEM),) * 2,
    )(fresh, penalty)


def solution(mesh):
    placed = (P(("pts", "cen"), None), P(), P(), P(), P("cen", None, None))
    return jax.shard_map(
        functools.partial(body, mesh.shape["pts"], mesh.shape["cen"]),
        mesh=mesh,
        in_specs=placed,
        out_specs=(P("cen", "pts", None), P(("pts", "cen"))),
        check_vma=False,
    )
```

profile of v0, /device:TPU:0, one launch (start us, length us, event | category | flops | bytes accessed | tf_op | source)
XLA Modules:
  0.0 42.5 jit_solution(10754697411719536816)
XLA Ops:
  0.6 40.2 %shard_map.68 = (f32[256,256]{1,0:T(8,128)}, f32[1,256]{1,0:T(1,128)}) custom-call(bf16[256,512]{1,0:T(8,128)(2,1)} %states_hbm.1, bf16[512,1024]{1,0:T(8,128)(2,1)} %first_hbm.1, f32[1024]{0:T(1024)} %bias_ref.1, bf16[1024,256]{1,0:T(8,128)(2,1)} %second_hbm.1, bf16[1,4096,256]{2,1,0:T(8,128)(2,1)} %cen_hbm.1), custom_call_target="tpu_custom_call" | custom-call | tf_op jit(solution)/shard_map/pallas_call | solution.py:316
  40.8 1.7 %shard_map.69 = (f32[1,256,256]{2,1,0:T(8,128)}, f32[256]{0:T(256)}) custom-call(f32[256,256]{1,0:T(8,128)} %get-tuple-element.4.fresh_ref, f32[1,256]{1,0:T(1,128)} %get-tuple-element.5.pen_ref), custom_call_target="tpu_custom_call" | custom-call | tf_op jit(solution)/shard_map/pallas_call | solution.py:361
where the time goes:
time: 42.7 us; the launch traced here: 42.5 us
  Pallas kernels  41.8 us (98%)
  between operations  0.64 us (1%)
    pallas_call x1, Pallas kernels, body(): pl.pallas_call(functools.partial(kernel, n_pts, n_cen), out_shape=(jax.Sh...  40.2 us
    pallas_call x1, Pallas kernels, body(): pl.pallas_call(finish, out_shape=(jax.ShapeDtypeStruct((1, owned, width),...  1.68 us

commit v1 on v0

v1 whole, which is shorter than its diff:
```python
import functools
import math

import jax
import jax.numpy as jnp
from jax import lax
from jax.experimental import pallas as pl
from jax.experimental.pallas import tpu as pltpu
from jax.sharding import PartitionSpec as P

smoothing_scale = 16.0
LOG2E = math.log2(math.e)
MESH = pl.DeviceIdType.MESH
NT = (((1,), (1,)), ((), ()))
PIECES = 4
HALF = PIECES // 2


def kernel(
    n_pts, n_cen, states_hbm, first_hbm, bias_hbm, second_hbm, cen_hbm, out_ref, pen_ref,
    states_ref, first_ref, bias_ref, second_ref, cen_ref, load_sem,
    allc, stat, norm, squares, weighted, counts, other_sums, other_counts,
    line_sem, c_sem, c_rest, x_sem, x_rest, d_sem, stat_sem, norm_sem, pair_sem,
    send_up, send_down, send_x, send_c, send_stat, send_norm, send_pair, token,
):
    n, width = states_ref.shape[0], second_ref.shape[1]
    n_z, others = n_pts // 4, n_cen - 1
    n_own = out_ref.shape[0]
    piece = n // PIECES

    def load(i, src, dst):
        return pltpu.make_async_copy(src, dst, load_sem.at[i])

    load_states = load(0, states_hbm, states_ref)
    load_first = load(1, first_hbm, first_ref)
    load_bias = load(2, bias_hbm, bias_ref)
    load_second = load(3, second_hbm, second_ref)
    load_cen = load(4, cen_hbm.at[0], cen_ref)
    for copy in (load_states, load_first, load_bias, load_second):
        copy.start()

    p, c = lax.axis_index("pts"), lax.axis_index("cen")
    core, x, z = lax.rem(p, 2), lax.rem(p // 2, 2), p // 4
    has_up, has_down = z < n_z - 1, z > 0

    def at(zi, xi, ki):
        return (zi * 2 + xi) * 2 + ki

    def c_at(j):
        return lax.rem(c + j, n_cen)

    def block(zi, xi, ci):
        return (zi * 2 + xi) * n_cen + ci

    up_peer = (at(lax.rem(z + 1, n_z), x, core), c)
    down_peer = (at(lax.rem(z + n_z - 1, n_z), x, core), c)
    x_peer = (at(z, 1 - x, core), c)
    core_peer = (at(z, x, 1 - core), c)
    mine = block(z, x, c)

    barrier = pltpu.get_barrier_semaphore()

    def greet(peer):
        pl.semaphore_signal(barrier, inc=1, device_id=peer, device_id_type=MESH)

    pl.when(has_up)(lambda: greet(up_peer))
    pl.when(has_down)(lambda: greet(down_peer))
    greet(x_peer)
    greet(core_peer)
    for j in range(1, n_cen):
        greet((p, c_at(j)))
    greetings = 2 + others + has_up.astype(jnp.int32) + has_down.astype(jnp.int32)

    def rows_of(q, count=1):
        return pl.ds(q * piece, count * piece)

    def remote(src, dst, send, recv, peer):
        return pltpu.make_async_remote_copy(
            src_ref=src, dst_ref=dst, send_sem=send, recv_sem=recv,
            device_id=peer, device_id_type=MESH,
        )

    def send(b, q, send_sem, recv_sem, peer):
        ref = allc.at[b, rows_of(q)]
        remote(ref, ref, send_sem, recv_sem, peer).start()

    def arrived(ref, recv_sem):
        remote(ref, ref, send_x, recv_sem, core_peer).wait_recv()

    def seat(zi, j):
        return zi * others + j - 1

    def c_slot(zi, j, q):
        return c_sem.at[seat(zi, j), q] if q < HALF else c_rest.at[seat(zi, j)]

    def x_slot(zi, q):
        return x_rest.at[zi] if q < HALF else x_sem.at[zi, q - HALF]

    def at_distance(d, visit):
        if d == 0:
            visit(z)
            return
        pl.when(z + d < n_z)(lambda: visit(z + d))
        pl.when(z >= d)(lambda: visit(z - d))

    def spread(zi, q):
        b = block(zi, x, c)
        pl.when(jnp.logical_and(has_up, zi <= z))(
            lambda: send(b, q, send_up, line_sem.at[zi, q], up_peer)
        )
        pl.when(jnp.logical_and(has_down, zi >= z))(
            lambda: send(b, q, send_down, line_sem.at[zi, q], down_peer)
        )
        for j in range(1, n_cen):
            send(b, q, send_c, c_slot(zi, n_cen - j, q), (p, c_at(j)))
        send(b, q, send_x, x_slot(zi, q), x_peer)

    def line_step(d, q):
        def visit(zi):
            arrived(allc.at[block(zi, x, c), rows_of(q)], line_sem.at[zi, q])
            spread(zi, q)

        at_distance(d, visit)

    def cross_step(d, q):
        def visit(zi):
            if q < HALF:
                for j in range(1, n_cen):
                    b = block(zi, x, c_at(j))
                    arrived(allc.at[b, rows_of(q)], c_slot(zi, j, q))
                    send(b, q, send_x, d_sem.at[seat(zi, j)], x_peer)
            else:
                b = block(zi, 1 - x, c)
                arrived(allc.at[b, rows_of(q)], x_slot(zi, q))
                for j in range(1, n_cen):
                    send(b, q, send_c, d_sem.at[seat(zi, n_cen - j)], (p, c_at(j)))

        at_distance(d, visit)

    with jax.named_scope("load"):
        load_states.wait()
        load_first.wait()
        load_bias.wait()
        load_cen.start()
    part = n // 2
    for h in range(2):
        rows = pl.ds(h * part, part)
        with jax.named_scope(f"encode{h}"):
            pre = jnp.dot(states_ref[rows, :], first_ref[...], preferred_element_type=jnp.float32)
            hidden = jax.nn.gelu(pre + bias_ref[...][None, :]).astype(jnp.bfloat16)
            if h == 0:
                load_second.wait()
            allc[mine, rows, :] = jnp.dot(
                hidden, second_ref[...], preferred_element_type=jnp.float32
            ).astype(jnp.bfloat16)
        if h == 0:
            with jax.named_scope("barrier"):
                pl.semaphore_wait(barrier, greetings)
        for q in range(h * HALF, (h + 1) * HALF):
            spread(z, q)

    def tell(i, peer):
        pl.semaphore_signal(token.at[i], inc=1, device_id=peer, device_id_type=MESH)

    pl.when(z == 0)(lambda: tell(0, up_peer))
    pl.when(z == n_z - 1)(lambda: tell(1, down_peer))

    def pass_on(s):
        @pl.when(jnp.logical_and(has_down, z == s + 1))
        def _():
            pl.semaphore_wait(token.at[0], 1)
            pl.when(has_up)(lambda: tell(0, up_peer))

        @pl.when(jnp.logical_and(has_up, 2 * (n_z - 2 - z) == s))
        def _():
            pl.semaphore_wait(token.at[1], 1)
            pl.when(has_down)(lambda: tell(1, down_peer))

        if s == 2 * (n_z - 2):
            tell(2, x_peer)

    tile = min(512, cen_ref.shape[0])
    tiles = cen_ref.shape[0] // tile
    scale = 2.0 * LOG2E / smoothing_scale

    def tile_rows(i):
        return pl.ds(pl.multiple_of(i * tile, tile), tile)

    def square_step(i, _):
        wide = cen_ref[tile_rows(i), :].astype(jnp.float32)
        total = jnp.sum(wide * wide, axis=1, keepdims=True) * (LOG2E / smoothing_scale)
        squares[tile_rows(i), :] = jnp.broadcast_to(total, (tile, 128))
        return 0

    def less_squares(scores, rows):
        offset = squares[rows, :]
        return jnp.concatenate(
            [scores[:, q * 128:(q + 1) * 128] * scale - offset for q in range(scores.shape[1] // 128)],
            axis=1,
        )

    def stats_step(b, i, carry):
        peak, total = carry
        scores = lax.dot_general(
            cen_ref[tile_rows(i), :], allc[b], NT, preferred_element_type=jnp.float32
        )
        scores = less_squares(scores, tile_rows(i)).reshape(tile // 8, 8, n)
        peak_next = jnp.maximum(peak, jnp.max(scores, axis=0))
        total_next = total * jnp.exp2(peak - peak_next) + jnp.sum(
            jnp.exp2(scores - peak_next[None]), axis=0
        )
        return peak_next, total_next

    group_rows = n * n_cen

    def keep_stats(j, carry):
        peak, total = carry
        top = jnp.max(peak, axis=0, keepdims=True)
        mass = jnp.sum(total * jnp.exp2(peak - top), axis=0, keepdims=True)
        start = pl.multiple_of(c_at(j) * n, n)
        stat[c, :, pl.ds(start, n)] = top
        stat[c, :, pl.ds(group_rows + start, n)] = mass

    fresh = (jnp.full((8, n), -jnp.inf, jnp.float32), jnp.zeros((8, n), jnp.float32))

    with jax.named_scope("squares"):
        load_cen.wait()
        lax.fori_loop(0, tiles, square_step, 0)
    with jax.named_scope("stats_own"):
        keep_stats(0, lax.fori_loop(0, tiles, functools.partial(stats_step, mine), fresh))
    wide = allc[mine].astype(jnp.float32)
    lengths = lax.dot_general(
        jnp.ones((8, width), jnp.float32), wide * wide, NT,
        preferred_element_type=jnp.float32, precision=lax.Precision.HIGHEST,
    )
    weighted[...] = jnp.zeros_like(weighted)
    counts[...] = jnp.zeros_like(counts)

    pair = pl.ds(pl.multiple_of((p - core) * n_own, 2 * n_own), 2 * n_own)

    def consume(b, g, ci):
        rows = allc[b]
        scores = lax.dot_general(cen_ref[pair, :], rows, NT, preferred_element_type=jnp.float32)
        level = norm[g, :, pl.ds(pl.multiple_of(ci * n, n), n)]
        resp = jnp.exp2(less_squares(scores, pair) - level)
        lanes = resp[:, 0:128]
        for q in range(1, n // 128):
            lanes = lanes + resp[:, q * 128:(q + 1) * 128]
        counts[...] += lanes.reshape(counts.shape)
        weighted[...] += jnp.dot(
            resp.astype(jnp.bfloat16), rows, preferred_element_type=jnp.float32
        ).reshape(weighted.shape)

    def ordered(i):
        near = jnp.minimum(z, n_z - 1 - z)
        beside = z + (i + 1) // 2 if i % 2 else z - i // 2
        beyond = jnp.where(z <= n_z - 1 - z, i, n_z - 1 - i)
        return jnp.where(i <= 2 * near, beside, beyond)

    def rest_of(b, q, sem):
        arrived(allc.at[b, rows_of(q, HALF)], sem)

    def norm_arrived(zi, xi):
        g = zi * 2 + xi
        arrived(norm.at[g], norm_sem.at[g])

    def take_line(i):
        zi = ordered(i)
        if i > 0:
            norm_arrived(zi, x)
        consume(block(zi, x, c), zi * 2 + x, c)

    def take_c(i):
        zi = ordered(i)

        def one(j, _):
            b = block(zi, x, c_at(j))
            if i > 0:
                rest_of(b, HALF, c_rest.at[seat(zi, j)])
            consume(b, zi * 2 + x, c_at(j))
            return 0

        lax.fori_loop(1, n_cen, one, 0, unroll=others == 1)

    def take_x(i):
        zi = ordered(i)
        norm_arrived(zi, 1 - x)
        rest_of(block(zi, 1 - x, c), 0, x_rest.at[zi])
        consume(block(zi, 1 - x, c), zi * 2 + 1 - x, c)

    def take_d(i):
        zi = ordered(i)

        def one(j, _):
            b = block(zi, 1 - x, c_at(j))
            arrived(allc.at[b], d_sem.at[seat(zi, j)])
            consume(b, zi * 2 + 1 - x, c_at(j))
            return 0

        lax.fori_loop(1, n_cen, one, 0, unroll=others == 1)

    def stats_cross(first, last, carry):
        nxt = []
        for j in range(1, n_cen):
            step = functools.partial(stats_step, block(z, x, c_at(j)))
            nxt.append(lax.fori_loop(first, last, step, carry[j - 1]))
        return nxt

    def share_stats():
        for j in range(1, n_cen):
            remote(
                stat.at[c], stat.at[c], send_stat, stat_sem.at[n_cen - j - 1], (p, c_at(j))
            ).start()

    def share_norm():
        for j in range(1, n_cen):
            s = c_at(j)
            arrived(stat.at[s], stat_sem.at[j - 1])
        top = stat[0, :, 0:group_rows]
        for s in range(1, n_cen):
            top = jnp.maximum(top, stat[s, :, 0:group_rows])
        mass = jnp.zeros_like(top)
        for s in range(n_cen):
            mass = mass + stat[s, :, group_rows:2 * group_rows] * jnp.exp2(
                stat[s, :, 0:group_rows] - top
            )
        level = top + jnp.log(mass) * LOG2E
        g = z * 2 + x
        norm[g] = level
        pl.semaphore_wait(token.at[2], 1)
        for k in range(1, 2 * n_z):
            h = lax.rem(g + k, 2 * n_z)
            remote(norm.at[g], norm.at[g], send_norm, norm_sem.at[g], (h * 2 + core, c)).start()
        own = norm[g, :, pl.ds(pl.multiple_of(c * n, n), n)]
        pen_ref[...] = (-(smoothing_scale / width)) * (
            own * math.log(2.0) - lengths[0:1, :] / smoothing_scale
        )

    tasks = []
    for i in range(n_z):
        tasks += [
            functools.partial(take_line, i), functools.partial(take_c, i),
            functools.partial(take_x, i), functools.partial(take_d, i),
        ]
    if n_z > 1:
        swap = tasks[-6:]
        tasks[-6:] = [swap[0], swap[2], swap[1], swap[3], swap[4], swap[5]]
    total_steps = n_z * PIECES
    first_take = 2 * PIECES + 2
    carry = [fresh] * others
    done = 0
    for s in range(total_steps):
        d, q = 1 + s // PIECES, s % PIECES
        with jax.named_scope(f"move{s}"):
            if d < n_z:
                line_step(d, q)
            cross_step(d - 1, q)
            if s <= max(n_z - 2, 2 * (n_z - 2)):
                pass_on(s)
        with jax.named_scope(f"work{s}"):
            if s == PIECES - 1:
                for j in range(1, n_cen):
                    rest_of(block(z, x, c_at(j)), HALF, c_rest.at[seat(z, j)])
            if PIECES <= s < 2 * PIECES:
                k = s - PIECES
                carry = stats_cross(tiles * k // PIECES, tiles * (k + 1) // PIECES, carry)
            if s == 2 * PIECES - 1:
                for j in range(1, n_cen):
                    keep_stats(j, carry[j - 1])
                share_stats()
            if s == 2 * PIECES + 1:
                share_norm()
            if s >= first_take:
                until = len(tasks) * (s - first_take + 1) // (total_steps - first_take + 2)
                for task in tasks[done:until]:
                    task()
                done = until
    with jax.named_scope("tail"):
        for task in tasks[done:]:
            task()

    with jax.named_scope("pair"):
        sums = remote(
            weighted.at[1 - core], other_sums, send_pair.at[0], pair_sem.at[0], core_peer
        )
        tally = remote(
            counts.at[1 - core], other_counts, send_pair.at[1], pair_sem.at[1], core_peer
        )
        tally.start()
        sums.start()
        own_rows = pl.ds(pl.multiple_of(p * n_own, n_own), n_own)
        tally.wait()
        share = 1.0 / (
            jnp.sum(counts[core] + other_counts[...], axis=1, keepdims=True) + 1.0
        )
        sums.wait()
    with jax.named_scope("final"):
        out_ref[...] = (
            weighted[core] + other_sums[...] + cen_ref[own_rows, :].astype(jnp.float32)
        ) * share

    with jax.named_scope("sent"):

        def left(ref, send_sem):
            remote(ref, ref, send_sem, pair_sem.at[0], core_peer).wait_send()

        across = n_z + n_z * others // 2
        left(allc.at[pl.ds(0, across)], send_x)
        left(allc.at[pl.ds(0, others * (n_z + n_z // 2))], send_c)
        for zi in range(n_z - 1):
            pl.when(z == zi)(lambda zi=zi: left(allc.at[pl.ds(0, zi + 1)], send_up))
            pl.when(z == n_z - 1 - zi)(lambda zi=zi: left(allc.at[pl.ds(0, zi + 1)], send_down))
        left(stat.at[pl.ds(0, others)], send_stat)
        left(norm.at[pl.ds(0, 2 * n_z - 1)], send_norm)


def finish(fresh_ref, pen_ref, out_ref, cost_ref):
    out_ref[0] = fresh_ref[...]
    cost_ref[...] = pen_ref[0]


def body(n_pts, n_cen, states, first_weight, first_bias, second_weight, centroids):
    n, width = states.shape[0], second_weight.shape[1]
    k_dev = centroids.shape[1]
    owned = k_dev // n_pts
    n_z, others = n_pts // 4, n_cen - 1
    dma = pltpu.SemaphoreType.DMA
    vmem, f32 = pltpu.VMEM, jnp.float32
    args = [
        pltpu.with_memory_space_constraint(v, pltpu.HBM)
        for v in (states, first_weight, first_bias, second_weight, centroids)
    ]
    fresh, penalty = pl.pallas_call(
        functools.partial(kernel, n_pts, n_cen),
        out_shape=(vmem((owned, width), f32), vmem((1, n), f32)),
        in_specs=[pl.BlockSpec(memory_space=pltpu.HBM)] * 5,
        out_specs=(pl.BlockSpec(memory_space=vmem),) * 2,
        scratch_shapes=[
            vmem(states.shape, states.dtype),
            vmem(first_weight.shape, first_weight.dtype),
            vmem(first_bias.shape, first_bias.dtype),
            vmem(second_weight.shape, second_weight.dtype),
            vmem(centroids.shape[1:], centroids.dtype),
            dma((5,)),
            vmem((2 * n_z * n_cen, n, width), jnp.bfloat16),
            vmem((n_cen, 1, 2 * n_cen * n), f32),
            vmem((2 * n_z, 1, n_cen * n), f32),
            vmem((k_dev, 128), f32),
            vmem((2, owned, width), f32),
            vmem((2, owned, 128), f32),
            vmem((owned, width), f32),
            vmem((owned, 128), f32),
            dma((n_z, PIECES)),
            dma((n_z * others, HALF)),
            dma((n_z * others,)),
            dma((n_z, HALF)),
            dma((n_z,)),
            dma((n_z * others,)),
            dma((others,)),
            dma((2 * n_z,)),
            dma((2,)),
            dma, dma, dma, dma, dma, dma,
            dma((2,)),
            pltpu.SemaphoreType.REGULAR((3,)),
        ],
        compiler_params=pltpu.CompilerParams(
            collective_id=0, has_side_effects=True, vmem_limit_bytes=48 * 1024 * 1024
        ),
    )(*args)
    return pl.pallas_call(
        finish,
        out_shape=(
            jax.ShapeDtypeStruct((1, owned, width), f32),
            jax.ShapeDtypeStruct((n,), f32),
        ),
        in_specs=[pl.BlockSpec(memory_space=vmem)] * 2,
        out_specs=(pl.BlockSpec(memory_space=vmem),) * 2,
        compiler_params=pltpu.CompilerParams(vmem_limit_bytes=4 * 1024 * 1024),
    )(fresh, penalty)


def solution(mesh):
    placed = (P(("pts", "cen"), None), P(), P(), P(), P("cen", None, None))
    return jax.shard_map(
        functools.partial(body, mesh.shape["pts"], mesh.shape["cen"]),
        mesh=mesh,
        in_specs=placed,
        out_specs=(P("cen", "pts", None), P(("pts", "cen"))),
        check_vma=False,
    )
```

time: 42.7 us -> 35.8 us (0.84)
  Pallas kernels: 41.8 us -> 35 us
    pallas_call x1, Pallas kernels: 40.2 us -> 34.3 us  [body(): pl.pallas_call(functools.partial(kernel, n_pts, n_cen), out_shape=(vmem((...]
    pallas_call x1, Pallas kernels: 1.68 us -> 0.72 us  [body(): pl.pallas_call(finish, out_shape=(jax.ShapeDtypeStruct((1, owned, width),...]
where the time goes in v1:
time: 35.8 us; the launch traced here: 35.7 us
  Pallas kernels  35 us (98%)
  between operations  0.64 us (2%)
    pallas_call x1, Pallas kernels, body(): pl.pallas_call(functools.partial(kernel, n_pts, n_cen), out_shape=(vmem((...  34.3 us
    pallas_call x1, Pallas kernels, body(): pl.pallas_call(finish, out_shape=(jax.ShapeDtypeStruct((1, owned, width),...  0.72 us

profile of v1, /device:TPU:0, one launch (start us, length us, event | category | flops | bytes accessed | tf_op | source)
XLA Modules:
  0.0 35.7 jit_solution(7862948944257813231)
XLA Ops:
  0.6 34.3 %shard_map.68 = (f32[256,256]{1,0:T(8,128)S(1)}, f32[1,256]{1,0:T(1,128)S(1)}) custom-call(bf16[256,512]{1,0:T(8,128)(2,1)} %states_hbm.1, bf16[512,1024]{1,0:T(8,128)(2,1)} %first_hbm.1, f32[1024]{0:T(1024)} %bias_hbm.1, bf16[1024,256]{1,0:T(8,128)(2,1)} %second_hbm.1, bf16[1,4096,256]{2,1,0:T(8,128)(2,1)} %cen_hbm.1), custom_call_target="tpu_custom_call" | custom-call | tf_op jit(solution)/shard_map/pallas_call | solution.py:433
  34.9 0.7 %shard_map.69 = (f32[1,256,256]{2,1,0:T(8,128)}, f32[256]{0:T(256)}) custom-call(f32[256,256]{1,0:T(8,128)S(1)} %get-tuple-element.4.fresh_ref, f32[1,256]{1,0:T(1,128)S(1)} %get-tuple-element.5.pen_ref), custom_call_target="tpu_custom_call" | custom-call | tf_op jit(solution)/shard_map/pallas_call | solution.py:470

commit v2 on v1

--- a/solution.py
+++ b/solution.py
@@ -103,7 +103,7 @@
         pl.when(z + d < n_z)(lambda: visit(z + d))
         pl.when(z >= d)(lambda: visit(z - d))
 
-    def spread(zi, q):
+    def along(zi, q):
         b = block(zi, x, c)
         pl.when(jnp.logical_and(has_up, zi <= z))(
             lambda: send(b, q, send_up, line_sem.at[zi, q], up_peer)
@@ -111,6 +111,9 @@
         pl.when(jnp.logical_and(has_down, zi >= z))(
             lambda: send(b, q, send_down, line_sem.at[zi, q], down_peer)
         )
+
+    def aside(zi, q):
+        b = block(zi, x, c)
         for j in range(1, n_cen):
             send(b, q, send_c, c_slot(zi, n_cen - j, q), (p, c_at(j)))
         send(b, q, send_x, x_slot(zi, q), x_peer)
@@ -118,24 +121,28 @@
     def line_step(d, q):
         def visit(zi):
             arrived(allc.at[block(zi, x, c), rows_of(q)], line_sem.at[zi, q])
-            spread(zi, q)
+            along(zi, q)
 
         at_distance(d, visit)
 
-    def cross_step(d, q):
-        def visit(zi):
-            if q < HALF:
-                for j in range(1, n_cen):
-                    b = block(zi, x, c_at(j))
-                    arrived(allc.at[b, rows_of(q)], c_slot(zi, j, q))
-                    send(b, q, send_x, d_sem.at[seat(zi, j)], x_peer)
-            else:
-                b = block(zi, 1 - x, c)
-                arrived(allc.at[b, rows_of(q)], x_slot(zi, q))
-                for j in range(1, n_cen):
-                    send(b, q, send_c, d_sem.at[seat(zi, n_cen - j)], (p, c_at(j)))
-
-        at_distance(d, visit)
+    def ordered(i):
+        near = jnp.minimum(z, n_z - 1 - z)
+        beside = z + (i + 1) // 2 if i % 2 else z - i // 2
+        beyond = jnp.where(z <= n_z - 1 - z, i, n_z - 1 - i)
+        return jnp.where(i <= 2 * near, beside, beyond)
+
+    def cross_step(i, q):
+        zi = ordered(i)
+        if q < HALF:
+            for j in range(1, n_cen):
+                b = block(zi, x, c_at(j))
+                arrived(allc.at[b, rows_of(q)], c_slot(zi, j, q))
+                send(b, q, send_x, d_sem.at[seat(zi, j)], x_peer)
+        else:
+            b = block(zi, 1 - x, c)
+            arrived(allc.at[b, rows_of(q)], x_slot(zi, q))
+            for j in range(1, n_cen):
+                send(b, q, send_c, d_sem.at[seat(zi, n_cen - j)], (p, c_at(j)))
 
     with jax.named_scope("load"):
         load_states.wait()
@@ -157,7 +164,8 @@
             with jax.named_scope("barrier"):
                 pl.semaphore_wait(barrier, greetings)
         for q in range(h * HALF, (h + 1) * HALF):
-            spread(z, q)
+            along(z, q)
+            aside(z, q)
 
     def tell(i, peer):
         pl.semaphore_signal(token.at[i], inc=1, device_id=peer, device_id_type=MESH)
@@ -184,13 +192,12 @@
     scale = 2.0 * LOG2E / smoothing_scale
 
     def tile_rows(i):
-        return pl.ds(pl.multiple_of(i * tile, tile), tile)
-
-    def square_step(i, _):
+        return pl.ds(i * tile, tile) if isinstance(i, int) else pl.ds(pl.multiple_of(i * tile, tile), tile)
+
+    def square_step(i):
         wide = cen_ref[tile_rows(i), :].astype(jnp.float32)
         total = jnp.sum(wide * wide, axis=1, keepdims=True) * (LOG2E / smoothing_scale)
         squares[tile_rows(i), :] = jnp.broadcast_to(total, (tile, 128))
-        return 0
 
     def less_squares(scores, rows):
         offset = squares[rows, :]
@@ -223,11 +230,14 @@
 
     fresh = (jnp.full((8, n), -jnp.inf, jnp.float32), jnp.zeros((8, n), jnp.float32))
 
-    with jax.named_scope("squares"):
+    with jax.named_scope("cen"):
         load_cen.wait()
-        lax.fori_loop(0, tiles, square_step, 0)
     with jax.named_scope("stats_own"):
-        keep_stats(0, lax.fori_loop(0, tiles, functools.partial(stats_step, mine), fresh))
+        running = fresh
+        for i in range(tiles):
+            square_step(i)
+            running = stats_step(mine, i, running)
+        keep_stats(0, running)
     wide = allc[mine].astype(jnp.float32)
     lengths = lax.dot_general(
         jnp.ones((8, width), jnp.float32), wide * wide, NT,
@@ -238,24 +248,30 @@
 
     pair = pl.ds(pl.multiple_of((p - core) * n_own, 2 * n_own), 2 * n_own)
 
-    def consume(b, g, ci):
-        rows = allc[b]
+    def consume(b, g, ci, count=1):
+        span = count * n
+        rows = allc[pl.ds(b, count)].reshape(span, width)
         scores = lax.dot_general(cen_ref[pair, :], rows, NT, preferred_element_type=jnp.float32)
-        level = norm[g, :, pl.ds(pl.multiple_of(ci * n, n), n)]
+        level = norm[g, :, pl.ds(pl.multiple_of(ci * n, n), span)]
         resp = jnp.exp2(less_squares(scores, pair) - level)
         lanes = resp[:, 0:128]
-        for q in range(1, n // 128):
+        for q in range(1, span // 128):
             lanes = lanes + resp[:, q * 128:(q + 1) * 128]
         counts[...] += lanes.reshape(counts.shape)
         weighted[...] += jnp.dot(
             resp.astype(jnp.bfloat16), rows, preferred_element_type=jnp.float32
         ).reshape(weighted.shape)
 
-    def ordered(i):
-        near = jnp.minimum(z, n_z - 1 - z)
-        beside = z + (i + 1) // 2 if i % 2 else z - i // 2
-        beyond = jnp.where(z <= n_z - 1 - z, i, n_z - 1 - i)
-        return jnp.where(i <= 2 * near, beside, beyond)
+    def consume_group(g):
+        if n_cen <= 2:
+            consume(g * n_cen, g, 0, n_cen)
+            return
+
+        def one(ci, _):
+            consume(g * n_cen + ci, g, ci)
+            return 0
+
+        lax.fori_loop(0, n_cen, one, 0)
 
     def rest_of(b, q, sem):
         arrived(allc.at[b, rows_of(q, HALF)], sem)
@@ -268,27 +284,28 @@
         zi = ordered(i)
         if i > 0:
             norm_arrived(zi, x)
-        consume(block(zi, x, c), zi * 2 + x, c)
-
-    def take_c(i):
-        zi = ordered(i)
-
-        def one(j, _):
-            b = block(zi, x, c_at(j))
-            if i > 0:
-                rest_of(b, HALF, c_rest.at[seat(zi, j)])
-            consume(b, zi * 2 + x, c_at(j))
-            return 0
-
-        lax.fori_loop(1, n_cen, one, 0, unroll=others == 1)
-
-    def take_x(i):
+            for j in range(1, n_cen):
+                rest_of(block(zi, x, c_at(j)), HALF, c_rest.at[seat(zi, j)])
+        consume_group(zi * 2 + x)
+
+    def x_ready(i):
         zi = ordered(i)
         norm_arrived(zi, 1 - x)
         rest_of(block(zi, 1 - x, c), 0, x_rest.at[zi])
+
+    def take_x(i):
+        zi = ordered(i)
+        x_ready(i)
+        for j in range(1, n_cen):
+            arrived(allc.at[block(zi, 1 - x, c_at(j))], d_sem.at[seat(zi, j)])
+        consume_group(zi * 2 + 1 - x)
+
+    def take_last_b(i):
+        zi = ordered(i)
+        x_ready(i)
         consume(block(zi, 1 - x, c), zi * 2 + 1 - x, c)
 
-    def take_d(i):
+    def take_last_d(i):
         zi = ordered(i)
 
         def one(j, _):
@@ -303,7 +320,13 @@
         nxt = []
         for j in range(1, n_cen):
             step = functools.partial(stats_step, block(z, x, c_at(j)))
-            nxt.append(lax.fori_loop(first, last, step, carry[j - 1]))
+            running = carry[j - 1]
+            if n_cen <= 2:
+                for i in range(first, last):
+                    running = step(i, running)
+            else:
+                running = lax.fori_loop(first, last, step, running)
+            nxt.append(running)
         return nxt
 
     def share_stats():
@@ -336,48 +359,49 @@
             own * math.log(2.0) - lengths[0:1, :] / smoothing_scale
         )
 
-    tasks = []
+    total_steps = n_z * PIECES
+    cross_from, norm_at = PIECES, 2 * PIECES
+    takes = [functools.partial(take_line, 0)]
     for i in range(n_z):
-        tasks += [
-            functools.partial(take_line, i), functools.partial(take_c, i),
-            functools.partial(take_x, i), functools.partial(take_d, i),
-        ]
-    if n_z > 1:
-        swap = tasks[-6:]
-        tasks[-6:] = [swap[0], swap[2], swap[1], swap[3], swap[4], swap[5]]
-    total_steps = n_z * PIECES
-    first_take = 2 * PIECES + 2
+        if i > 0:
+            takes.append(functools.partial(take_line, i))
+        if i < n_z - 1:
+            takes.append(functools.partial(take_x, i))
+    takes += [functools.partial(take_last_b, n_z - 1), functools.partial(take_last_d, n_z - 1)]
+    first_take = norm_at + 1
+    held = 3
     carry = [fresh] * others
     done = 0
     for s in range(total_steps):
-        d, q = 1 + s // PIECES, s % PIECES
+        i, q = 1 + s // PIECES, s % PIECES
         with jax.named_scope(f"move{s}"):
-            if d < n_z:
-                line_step(d, q)
-            cross_step(d - 1, q)
+            if i < n_z:
+                line_step(i, q)
+                aside(ordered(i), q)
+            cross_step(i - 1, q)
             if s <= max(n_z - 2, 2 * (n_z - 2)):
                 pass_on(s)
         with jax.named_scope(f"work{s}"):
             if s == PIECES - 1:
                 for j in range(1, n_cen):
                     rest_of(block(z, x, c_at(j)), HALF, c_rest.at[seat(z, j)])
-            if PIECES <= s < 2 * PIECES:
-                k = s - PIECES
-                carry = stats_cross(tiles * k // PIECES, tiles * (k + 1) // PIECES, carry)
-            if s == 2 * PIECES - 1:
-                for j in range(1, n_cen):
-                    keep_stats(j, carry[j - 1])
-                share_stats()
-            if s == 2 * PIECES + 1:
+            if cross_from <= s < cross_from + 2:
+                k = s - cross_from
+                carry = stats_cross(tiles * k // 2, tiles * (k + 1) // 2, carry)
+                if k == 1:
+                    for j in range(1, n_cen):
+                        keep_stats(j, carry[j - 1])
+                    share_stats()
+            if s == norm_at:
                 share_norm()
             if s >= first_take:
-                until = len(tasks) * (s - first_take + 1) // (total_steps - first_take + 2)
-                for task in tasks[done:until]:
-                    task()
+                until = (len(takes) - held) * (s - first_take + 1) // (total_steps - first_take)
+                for take in takes[done:until]:
+                    take()
                 done = until
     with jax.named_scope("tail"):
-        for task in tasks[done:]:
-            task()
+        for take in takes[done:]:
+            take()
 
     with jax.named_scope("pair"):
         sums = remote(

time: 35.8 us -> 29.7 us (0.83)
  Pallas kernels: 35 us -> 28.9 us
    pallas_call x1, Pallas kernels: 34.3 us -> 28.2 us  [body(): pl.pallas_call(functools.partial(kernel, n_pts, n_cen), out_shape=(vmem((...]
where the time goes in v2:
time: 29.7 us; the launch traced here: 29.5 us
  Pallas kernels  28.9 us (97%)
  between operations  0.64 us (2%)
    pallas_call x1, Pallas kernels, body(): pl.pallas_call(functools.partial(kernel, n_pts, n_cen), out_shape=(vmem((...  28.2 us
    pallas_call x1, Pallas kernels, body(): pl.pallas_call(finish, out_shape=(jax.ShapeDtypeStruct((1, owned, width),...  0.72 us

profile of v2, /device:TPU:0, one launch (start us, length us, event | category | flops | bytes accessed | tf_op | source)
XLA Modules:
  0.0 29.5 jit_solution(12173390681618147015)
XLA Ops:
  0.6 28.2 %shard_map.68 = (f32[256,256]{1,0:T(8,128)S(1)}, f32[1,256]{1,0:T(1,128)S(1)}) custom-call(bf16[256,512]{1,0:T(8,128)(2,1)} %states_hbm.1, bf16[512,1024]{1,0:T(8,128)(2,1)} %first_hbm.1, f32[1024]{0:T(1024)} %bias_hbm.1, bf16[1024,256]{1,0:T(8,128)(2,1)} %second_hbm.1, bf16[1,4096,256]{2,1,0:T(8,128)(2,1)} %cen_hbm.1), custom_call_target="tpu_custom_call" | custom-call | tf_op jit(solution)/shard_map/pallas_call | solution.py:457
  28.8 0.7 %shard_map.69 = (f32[1,256,256]{2,1,0:T(8,128)}, f32[256]{0:T(256)}) custom-call(f32[256,256]{1,0:T(8,128)S(1)} %get-tuple-element.4.fresh_ref, f32[1,256]{1,0:T(1,128)S(1)} %get-tuple-element.5.pen_ref), custom_call_target="tpu_custom_call" | custom-call | tf_op jit(solution)/shard_map/pallas_call | solution.py:494

commit v3 on v2

--- a/solution.py
+++ b/solution.py
@@ -21,7 +21,8 @@
     states_ref, first_ref, bias_ref, second_ref, cen_ref, load_sem,
     allc, stat, norm, squares, weighted, counts, other_sums, other_counts,
     line_sem, c_sem, c_rest, x_sem, x_rest, d_sem, stat_sem, norm_sem, pair_sem,
-    send_up, send_down, send_x, send_c, send_stat, send_norm, send_pair, token,
+    send_up, send_down, send_x, send_c, send_dup, send_ddown, send_dx, send_dc,
+    send_stat, send_norm, send_pair, token,
 ):
     n, width = states_ref.shape[0], second_ref.shape[1]
     n_z, others = n_pts // 4, n_cen - 1
@@ -43,8 +44,10 @@
     core, x, z = lax.rem(p, 2), lax.rem(p // 2, 2), p // 4
     has_up, has_down = z < n_z - 1, z > 0
 
-    def at(zi, xi, ki):
-        return (zi * 2 + xi) * 2 + ki
+    side = lax.rem(core + x + z + c, 2)
+
+    def at(zi, xi, ci):
+        return ((zi * 2 + xi) * 2 + lax.rem(side + xi + zi + ci, 2), ci)
 
     def c_at(j):
         return lax.rem(c + j, n_cen)
@@ -52,10 +55,11 @@
     def block(zi, xi, ci):
         return (zi * 2 + xi) * n_cen + ci
 
-    up_peer = (at(lax.rem(z + 1, n_z), x, core), c)
-    down_peer = (at(lax.rem(z + n_z - 1, n_z), x, core), c)
-    x_peer = (at(z, 1 - x, core), c)
-    core_peer = (at(z, x, 1 - core), c)
+    def c_peer(j):
+        return at(z, x, c_at(j))
+
+    up_peer, down_peer = at(lax.rem(z + 1, n_z), x, c), at(lax.rem(z + n_z - 1, n_z), x, c)
+    x_peer, core_peer = at(z, 1 - x, c), (p + 1 - 2 * core, c)
     mine = block(z, x, c)
 
     barrier = pltpu.get_barrier_semaphore()
@@ -68,7 +72,7 @@
     greet(x_peer)
     greet(core_peer)
     for j in range(1, n_cen):
-        greet((p, c_at(j)))
+        greet(c_peer(j))
     greetings = 2 + others + has_up.astype(jnp.int32) + has_down.astype(jnp.int32)
 
     def rows_of(q, count=1):
@@ -105,25 +109,39 @@
 
     def along(zi, q):
         b = block(zi, x, c)
-        pl.when(jnp.logical_and(has_up, zi <= z))(
-            lambda: send(b, q, send_up, line_sem.at[zi, q], up_peer)
-        )
-        pl.when(jnp.logical_and(has_down, zi >= z))(
-            lambda: send(b, q, send_down, line_sem.at[zi, q], down_peer)
-        )
+        pl.when(passes_up(zi))(lambda: send(b, q, send_up, line_sem.at[zi, q], up_peer))
+        pl.when(passes_down(zi))(lambda: send(b, q, send_down, line_sem.at[zi, q], down_peer))
 
     def aside(zi, q):
         b = block(zi, x, c)
         for j in range(1, n_cen):
-            send(b, q, send_c, c_slot(zi, n_cen - j, q), (p, c_at(j)))
+            send(b, q, send_c, c_slot(zi, n_cen - j, q), c_peer(j))
         send(b, q, send_x, x_slot(zi, q), x_peer)
 
-    def line_step(d, q):
+    def passes_up(zi):
+        return jnp.logical_and(has_up, zi <= z)
+
+    def passes_down(zi):
+        return jnp.logical_and(has_down, zi >= z)
+
+    def passes(zi):
+        return jnp.logical_or(passes_up(zi), passes_down(zi))
+
+    def line_arrived(zi, q):
+        arrived(allc.at[block(zi, x, c), rows_of(q)], line_sem.at[zi, q])
+
+    def line_forward(d, q):
         def visit(zi):
-            arrived(allc.at[block(zi, x, c), rows_of(q)], line_sem.at[zi, q])
-            along(zi, q)
+            @pl.when(passes(zi))
+            def _():
+                line_arrived(zi, q)
+                along(zi, q)
 
         at_distance(d, visit)
+
+    def line_step(i, q):
+        zi = ordered(i)
+        pl.when(jnp.logical_not(passes(zi)))(lambda: line_arrived(zi, q))
 
     def ordered(i):
         near = jnp.minimum(z, n_z - 1 - z)
@@ -131,18 +149,55 @@
         beyond = jnp.where(z <= n_z - 1 - z, i, n_z - 1 - i)
         return jnp.where(i <= 2 * near, beside, beyond)
 
+    def d_slot(zi, j, q):
+        return d_sem.at[seat(zi, j), q]
+
+    def by_line(q):
+        return HALF - 1 <= q <= HALF
+
     def cross_step(i, q):
         zi = ordered(i)
-        if q < HALF:
-            for j in range(1, n_cen):
+
+        def forward(visit):
+            if i == 0:
+                visit()
+            elif not by_line(q):
+                pl.when(jnp.abs(zi - z) > 1)(visit)
+
+        for j in range(1, n_cen):
+            if q < HALF:
                 b = block(zi, x, c_at(j))
                 arrived(allc.at[b, rows_of(q)], c_slot(zi, j, q))
-                send(b, q, send_x, d_sem.at[seat(zi, j)], x_peer)
-        else:
+                forward(functools.partial(send, b, q, send_dx, d_slot(zi, j, q), x_peer))
+        if q >= HALF:
             b = block(zi, 1 - x, c)
             arrived(allc.at[b, rows_of(q)], x_slot(zi, q))
             for j in range(1, n_cen):
-                send(b, q, send_c, d_sem.at[seat(zi, n_cen - j)], (p, c_at(j)))
+                forward(
+                    functools.partial(send, b, q, send_dc, d_slot(zi, n_cen - j, q), c_peer(j))
+                )
+
+    def diagonal_step(d, q):
+        def visit(zi):
+            for j in range(1, n_cen):
+                b = block(zi, 1 - x, c_at(j))
+                slot = d_slot(zi, j, q)
+                up, down = passes_up(zi), passes_down(zi)
+                pl.when(jnp.logical_or(up, down))(
+                    functools.partial(arrived, allc.at[b, rows_of(q)], slot)
+                )
+                pl.when(up)(functools.partial(send, b, q, send_dup, slot, up_peer))
+                pl.when(down)(functools.partial(send, b, q, send_ddown, slot, down_peer))
+
+        at_distance(d, visit)
+
+    def corner_ready(zi, j):
+        b = block(zi, 1 - x, c_at(j))
+        for q in range(PIECES):
+            seen = passes(zi) if by_line(q) else zi == z
+            pl.when(jnp.logical_not(seen))(
+                functools.partial(arrived, allc.at[b, rows_of(q)], d_slot(zi, j, q))
+            )
 
     with jax.named_scope("load"):
         load_states.wait()
@@ -206,12 +261,12 @@
             axis=1,
         )
 
-    def stats_step(b, i, carry):
+    def stats_step(rows, i, carry):
         peak, total = carry
         scores = lax.dot_general(
-            cen_ref[tile_rows(i), :], allc[b], NT, preferred_element_type=jnp.float32
-        )
-        scores = less_squares(scores, tile_rows(i)).reshape(tile // 8, 8, n)
+            cen_ref[tile_rows(i), :], rows, NT, preferred_element_type=jnp.float32
+        )
+        scores = less_squares(scores, tile_rows(i)).reshape(tile // 8, 8, rows.shape[0])
         peak_next = jnp.maximum(peak, jnp.max(scores, axis=0))
         total_next = total * jnp.exp2(peak - peak_next) + jnp.sum(
             jnp.exp2(scores - peak_next[None]), axis=0
@@ -220,24 +275,25 @@
 
     group_rows = n * n_cen
 
-    def keep_stats(j, carry):
+    def keep_stats(j, first, carry):
         peak, total = carry
         top = jnp.max(peak, axis=0, keepdims=True)
         mass = jnp.sum(total * jnp.exp2(peak - top), axis=0, keepdims=True)
-        start = pl.multiple_of(c_at(j) * n, n)
-        stat[c, :, pl.ds(start, n)] = top
-        stat[c, :, pl.ds(group_rows + start, n)] = mass
-
-    fresh = (jnp.full((8, n), -jnp.inf, jnp.float32), jnp.zeros((8, n), jnp.float32))
+        start = pl.multiple_of(c_at(j) * n + first, 128)
+        stat[c, :, pl.ds(start, top.shape[1])] = top
+        stat[c, :, pl.ds(group_rows + start, top.shape[1])] = mass
+
+    def fresh(count):
+        return jnp.full((8, count), -jnp.inf, jnp.float32), jnp.zeros((8, count), jnp.float32)
 
     with jax.named_scope("cen"):
         load_cen.wait()
     with jax.named_scope("stats_own"):
-        running = fresh
+        running = fresh(n)
         for i in range(tiles):
             square_step(i)
-            running = stats_step(mine, i, running)
-        keep_stats(0, running)
+            running = stats_step(allc[mine], i, running)
+        keep_stats(0, 0, running)
     wide = allc[mine].astype(jnp.float32)
     lengths = lax.dot_general(
         jnp.ones((8, width), jnp.float32), wide * wide, NT,
@@ -246,21 +302,25 @@
     weighted[...] = jnp.zeros_like(weighted)
     counts[...] = jnp.zeros_like(counts)
 
-    pair = pl.ds(pl.multiple_of((p - core) * n_own, 2 * n_own), 2 * n_own)
-
-    def consume(b, g, ci, count=1):
+    both = pl.ds(pl.multiple_of((p - core) * n_own, 2 * n_own), 2 * n_own)
+
+    def consume(b, g, ci, count=1, owner=None):
         span = count * n
         rows = allc[pl.ds(b, count)].reshape(span, width)
+        pair, seats = both, slice(None)
+        if owner is not None:
+            pair = pl.ds(pl.multiple_of((p - core + owner) * n_own, n_own), n_own)
+            seats = pl.ds(owner, 1)
         scores = lax.dot_general(cen_ref[pair, :], rows, NT, preferred_element_type=jnp.float32)
         level = norm[g, :, pl.ds(pl.multiple_of(ci * n, n), span)]
         resp = jnp.exp2(less_squares(scores, pair) - level)
         lanes = resp[:, 0:128]
         for q in range(1, span // 128):
             lanes = lanes + resp[:, q * 128:(q + 1) * 128]
-        counts[...] += lanes.reshape(counts.shape)
-        weighted[...] += jnp.dot(
+        counts[seats] += lanes.reshape(-1, n_own, 128)
+        weighted[seats] += jnp.dot(
             resp.astype(jnp.bfloat16), rows, preferred_element_type=jnp.float32
-        ).reshape(weighted.shape)
+        ).reshape(-1, n_own, width)
 
     def consume_group(g):
         if n_cen <= 2:
@@ -280,59 +340,56 @@
         g = zi * 2 + xi
         arrived(norm.at[g], norm_sem.at[g])
 
-    def take_line(i):
+    def line_ready(i):
         zi = ordered(i)
         if i > 0:
             norm_arrived(zi, x)
             for j in range(1, n_cen):
                 rest_of(block(zi, x, c_at(j)), HALF, c_rest.at[seat(zi, j)])
-        consume_group(zi * 2 + x)
 
     def x_ready(i):
         zi = ordered(i)
         norm_arrived(zi, 1 - x)
         rest_of(block(zi, 1 - x, c), 0, x_rest.at[zi])
 
-    def take_x(i):
-        zi = ordered(i)
+    def cross_ready(i):
         x_ready(i)
         for j in range(1, n_cen):
-            arrived(allc.at[block(zi, 1 - x, c_at(j))], d_sem.at[seat(zi, j)])
-        consume_group(zi * 2 + 1 - x)
+            corner_ready(ordered(i), j)
+
+    def take_line(i):
+        consume_group(ordered(i) * 2 + x)
+
+    def take_cross(i):
+        consume_group(ordered(i) * 2 + 1 - x)
 
     def take_last_b(i):
         zi = ordered(i)
-        x_ready(i)
         consume(block(zi, 1 - x, c), zi * 2 + 1 - x, c)
 
-    def take_last_d(i):
+    def take_last_d(i, owner):
         zi = ordered(i)
-
-        def one(j, _):
-            b = block(zi, 1 - x, c_at(j))
-            arrived(allc.at[b], d_sem.at[seat(zi, j)])
-            consume(b, zi * 2 + 1 - x, c_at(j))
-            return 0
-
-        lax.fori_loop(1, n_cen, one, 0, unroll=others == 1)
-
-    def stats_cross(first, last, carry):
-        nxt = []
         for j in range(1, n_cen):
-            step = functools.partial(stats_step, block(z, x, c_at(j)))
-            running = carry[j - 1]
-            if n_cen <= 2:
-                for i in range(first, last):
-                    running = step(i, running)
-            else:
-                running = lax.fori_loop(first, last, step, running)
-            nxt.append(running)
-        return nxt
+            consume(block(zi, 1 - x, c_at(j)), zi * 2 + 1 - x, c_at(j), owner=owner)
+
+    def cross_stats(j, first):
+        b = block(z, x, c_at(j))
+
+        def step(i, carry):
+            return stats_step(allc[b, pl.ds(first, n // 2), :], i, carry)
+
+        running = fresh(n // 2)
+        if n_cen <= 2:
+            for i in range(tiles):
+                running = step(i, running)
+        else:
+            running = lax.fori_loop(0, tiles, step, running)
+        keep_stats(j, first, running)
 
     def share_stats():
         for j in range(1, n_cen):
             remote(
-                stat.at[c], stat.at[c], send_stat, stat_sem.at[n_cen - j - 1], (p, c_at(j))
+                stat.at[c], stat.at[c], send_stat, stat_sem.at[n_cen - j - 1], c_peer(j)
             ).start()
 
     def share_norm():
@@ -353,55 +410,70 @@
         pl.semaphore_wait(token.at[2], 1)
         for k in range(1, 2 * n_z):
             h = lax.rem(g + k, 2 * n_z)
-            remote(norm.at[g], norm.at[g], send_norm, norm_sem.at[g], (h * 2 + core, c)).start()
+            remote(norm.at[g], norm.at[g], send_norm, norm_sem.at[g], at(h // 2, lax.rem(h, 2), c)).start()
         own = norm[g, :, pl.ds(pl.multiple_of(c * n, n), n)]
         pen_ref[...] = (-(smoothing_scale / width)) * (
             own * math.log(2.0) - lengths[0:1, :] / smoothing_scale
         )
 
     total_steps = n_z * PIECES
-    cross_from, norm_at = PIECES, 2 * PIECES
-    takes = [functools.partial(take_line, 0)]
-    for i in range(n_z):
-        if i > 0:
-            takes.append(functools.partial(take_line, i))
-        if i < n_z - 1:
-            takes.append(functools.partial(take_x, i))
-    takes += [functools.partial(take_last_b, n_z - 1), functools.partial(take_last_d, n_z - 1)]
-    first_take = norm_at + 1
-    held = 3
-    carry = [fresh] * others
-    done = 0
+    norm_at, early_at = 2 * PIECES - 1, (n_z - 1) * PIECES - 1
+
+    diagonals = {}
+    for q in range(PIECES):
+        diagonals.setdefault(min(PIECES + 1 + (q + 1) // 2, total_steps - 1), []).append((0, q))
+    for d in range(1, n_z):
+        for e in range(2):
+            s = min(PIECES + 2 + 3 * d + e, total_steps - 1)
+            diagonals.setdefault(s, []).append((d, HALF - 1 + e))
     for s in range(total_steps):
         i, q = 1 + s // PIECES, s % PIECES
         with jax.named_scope(f"move{s}"):
             if i < n_z:
+                if i == 1:
+                    line_forward(1, q)
                 line_step(i, q)
                 aside(ordered(i), q)
+                if i > 1 and q < 2:
+                    for ahead in range(PIECES - 1) if q == 0 else (PIECES - 1,):
+                        line_forward(i, ahead)
             cross_step(i - 1, q)
+            for d, piece_index in diagonals.get(s, ()):
+                diagonal_step(d, piece_index)
             if s <= max(n_z - 2, 2 * (n_z - 2)):
                 pass_on(s)
         with jax.named_scope(f"work{s}"):
             if s == PIECES - 1:
                 for j in range(1, n_cen):
+                    cross_stats(j, 0)
                     rest_of(block(z, x, c_at(j)), HALF, c_rest.at[seat(z, j)])
-            if cross_from <= s < cross_from + 2:
-                k = s - cross_from
-                carry = stats_cross(tiles * k // 2, tiles * (k + 1) // 2, carry)
-                if k == 1:
-                    for j in range(1, n_cen):
-                        keep_stats(j, carry[j - 1])
-                    share_stats()
+                    cross_stats(j, n // 2)
+                share_stats()
             if s == norm_at:
                 share_norm()
-            if s >= first_take:
-                until = (len(takes) - held) * (s - first_take + 1) // (total_steps - first_take)
-                for take in takes[done:until]:
-                    take()
-                done = until
+                take_line(0)
+            if s == early_at:
+                line_ready(1)
+                take_line(1)
     with jax.named_scope("tail"):
-        for take in takes[done:]:
-            take()
+        last = n_z - 1
+        cross_ready(0)
+        for i in range(2, n_z):
+            line_ready(i)
+            if i < last:
+                cross_ready(i - 1)
+                take_cross(i - 2)
+                take_line(i)
+        cross_ready(last - 1)
+        x_ready(last)
+        take_cross(last - 2)
+        take_line(last)
+        take_cross(last - 1)
+        take_last_b(last)
+    with jax.named_scope("tail_d"):
+        for j in range(1, n_cen):
+            corner_ready(ordered(last), j)
+        take_last_d(last, 1 - core)
 
     with jax.named_scope("pair"):
         sums = remote(
@@ -412,6 +484,7 @@
         )
         tally.start()
         sums.start()
+        take_last_d(last, core)
         own_rows = pl.ds(pl.multiple_of(p * n_own, n_own), n_own)
         tally.wait()
         share = 1.0 / (
@@ -428,12 +501,27 @@
         def left(ref, send_sem):
             remote(ref, ref, send_sem, pair_sem.at[0], core_peer).wait_send()
 
-        across = n_z + n_z * others // 2
-        left(allc.at[pl.ds(0, across)], send_x)
-        left(allc.at[pl.ds(0, others * (n_z + n_z // 2))], send_c)
+        left(allc.at[pl.ds(0, n_z)], send_x)
+        left(allc.at[pl.ds(0, others * n_z)], send_c)
+
+        def left_corner(near):
+            corner = others * (HALF + (n_z - 1 - near) * (HALF - 1))
+            left(allc.at[pl.ds(0, corner), rows_of(0)], send_dx)
+            left(allc.at[pl.ds(0, corner), rows_of(0)], send_dc)
+
+        inside = jnp.logical_and(has_up, has_down)
+        pl.when(inside)(lambda: left_corner(2))
+        pl.when(jnp.logical_not(inside))(lambda: left_corner(1))
+
+        def left_line(count, whole, parts):
+            left(allc.at[pl.ds(0, count)], whole)
+            left(allc.at[pl.ds(0, (count + 1) * others), rows_of(0, 2)], parts)
+
         for zi in range(n_z - 1):
-            pl.when(z == zi)(lambda zi=zi: left(allc.at[pl.ds(0, zi + 1)], send_up))
-            pl.when(z == n_z - 1 - zi)(lambda zi=zi: left(allc.at[pl.ds(0, zi + 1)], send_down))
+            pl.when(z == zi)(functools.partial(left_line, zi + 1, send_up, send_dup))
+            pl.when(z == n_z - 1 - zi)(
+                functools.partial(left_line, zi + 1, send_down, send_ddown)
+            )
         left(stat.at[pl.ds(0, others)], send_stat)
         left(norm.at[pl.ds(0, 2 * n_z - 1)], send_norm)
 
@@ -479,11 +567,11 @@
             dma((n_z * others,)),
             dma((n_z, HALF)),
             dma((n_z,)),
-            dma((n_z * others,)),
+            dma((n_z * others, PIECES)),
             dma((others,)),
             dma((2 * n_z,)),
             dma((2,)),
-            dma, dma, dma, dma, dma, dma,
+            *([dma] * 10),
             dma((2,)),
             pltpu.SemaphoreType.REGULAR((3,)),
         ],

time: 29.7 us -> 27.3 us (0.919)
  Pallas kernels: 28.9 us -> 26.5 us
    pallas_call x1, Pallas kernels: 28.2 us -> 25.8 us  [body(): pl.pallas_call(functools.partial(kernel, n_pts, n_cen), out_shape=(vmem((...]
where the time goes in v3:
time: 27.3 us; the launch traced here: 27.1 us
  Pallas kernels  26.5 us (97%)
  between operations  0.64 us (2%)
    pallas_call x1, Pallas kernels, body(): pl.pallas_call(functools.partial(kernel, n_pts, n_cen), out_shape=(vmem((...  25.8 us
    pallas_call x1, Pallas kernels, body(): pl.pallas_call(finish, out_shape=(jax.ShapeDtypeStruct((1, owned, width),...  0.72 us

profile of v3, /device:TPU:0, one launch (start us, length us, event | category | flops | bytes accessed | tf_op | source)
XLA Modules:
  0.0 27.1 jit_solution(13058672321916074653)
XLA Ops:
  0.6 25.8 %shard_map.68 = (f32[256,256]{1,0:T(8,128)S(1)}, f32[1,256]{1,0:T(1,128)S(1)}) custom-call(bf16[256,512]{1,0:T(8,128)(2,1)} %states_hbm.1, bf16[512,1024]{1,0:T(8,128)(2,1)} %first_hbm.1, f32[1024]{0:T(1024)} %bias_hbm.1, bf16[1024,256]{1,0:T(8,128)(2,1)} %second_hbm.1, bf16[1,4096,256]{2,1,0:T(8,128)(2,1)} %cen_hbm.1), custom_call_target="tpu_custom_call" | custom-call | tf_op jit(solution)/shard_map/pallas_call | solution.py:545
  26.4 0.7 %shard_map.69 = (f32[1,256,256]{2,1,0:T(8,128)}, f32[256]{0:T(256)}) custom-call(f32[256,256]{1,0:T(8,128)S(1)} %get-tuple-element.4.fresh_ref, f32[1,256]{1,0:T(1,128)S(1)} %get-tuple-element.5.pen_ref), custom_call_target="tpu_custom_call" | custom-call | tf_op jit(solution)/shard_map/pallas_call | solution.py:582

commit v4 on v3

--- a/solution.py
+++ b/solution.py
@@ -14,15 +14,17 @@
 NT = (((1,), (1,)), ((), ()))
 PIECES = 4
 HALF = PIECES // 2
+LINE_PIECES = (0, HALF)
+ORDER = (1, 0, 3, 2)
 
 
 def kernel(
     n_pts, n_cen, states_hbm, first_hbm, bias_hbm, second_hbm, cen_hbm, out_ref, pen_ref,
-    states_ref, first_ref, bias_ref, second_ref, cen_ref, load_sem,
+    states_ref, first_ref, bias_ref, second_ref, cen_ref,
     allc, stat, norm, squares, weighted, counts, other_sums, other_counts,
-    line_sem, c_sem, c_rest, x_sem, x_rest, d_sem, stat_sem, norm_sem, pair_sem,
+    line_sem, c_sem, c_rest, x_sem, x_rest, d_sem, stat_sem, norm_sem,
     send_up, send_down, send_x, send_c, send_dup, send_ddown, send_dx, send_dc,
-    send_stat, send_norm, send_pair, token,
+    send_stat, send_norm, token,
 ):
     n, width = states_ref.shape[0], second_ref.shape[1]
     n_z, others = n_pts // 4, n_cen - 1
@@ -30,15 +32,23 @@
     piece = n // PIECES
 
     def load(i, src, dst):
-        return pltpu.make_async_copy(src, dst, load_sem.at[i])
+        return pltpu.make_async_copy(src, dst, (send_x, send_c, send_dx, send_dc, send_stat)[i])
 
     load_states = load(0, states_hbm, states_ref)
     load_first = load(1, first_hbm, first_ref)
     load_bias = load(2, bias_hbm, bias_ref)
     load_second = load(3, second_hbm, second_ref)
     load_cen = load(4, cen_hbm.at[0], cen_ref)
-    for copy in (load_states, load_first, load_bias, load_second):
-        copy.start()
+    def start(i, src, dst, parts):
+        rows = dst.shape[0] // parts
+        for k in range(parts):
+            at_rows = pl.ds(k * rows, rows)
+            load(i, src.at[at_rows], dst.at[at_rows]).start()
+
+    start(0, states_hbm, states_ref, 1)
+    start(1, first_hbm, first_ref, 4)
+    load_bias.start()
+    start(3, second_hbm, second_ref, 2)
 
     p, c = lax.axis_index("pts"), lax.axis_index("cen")
     core, x, z = lax.rem(p, 2), lax.rem(p // 2, 2), p // 4
@@ -153,7 +163,7 @@
         return d_sem.at[seat(zi, j), q]
 
     def by_line(q):
-        return HALF - 1 <= q <= HALF
+        return q in LINE_PIECES
 
     def cross_step(i, q):
         zi = ordered(i)
@@ -219,7 +229,7 @@
             with jax.named_scope("barrier"):
                 pl.semaphore_wait(barrier, greetings)
         for q in range(h * HALF, (h + 1) * HALF):
-            along(z, q)
+            along(z, ORDER[q])
             aside(z, q)
 
     def tell(i, peer):
@@ -275,11 +285,11 @@
 
     group_rows = n * n_cen
 
-    def keep_stats(j, first, carry):
+    def keep_stats(j, carry):
         peak, total = carry
         top = jnp.max(peak, axis=0, keepdims=True)
         mass = jnp.sum(total * jnp.exp2(peak - top), axis=0, keepdims=True)
-        start = pl.multiple_of(c_at(j) * n + first, 128)
+        start = pl.multiple_of(c_at(j) * n, n)
         stat[c, :, pl.ds(start, top.shape[1])] = top
         stat[c, :, pl.ds(group_rows + start, top.shape[1])] = mass
 
@@ -293,7 +303,7 @@
         for i in range(tiles):
             square_step(i)
             running = stats_step(allc[mine], i, running)
-        keep_stats(0, 0, running)
+        keep_stats(0, running)
     wide = allc[mine].astype(jnp.float32)
     lengths = lax.dot_general(
         jnp.ones((8, width), jnp.float32), wide * wide, NT,
@@ -322,13 +332,13 @@
             resp.astype(jnp.bfloat16), rows, preferred_element_type=jnp.float32
         ).reshape(-1, n_own, width)
 
-    def consume_group(g):
+    def consume_group(g, owner=None):
         if n_cen <= 2:
-            consume(g * n_cen, g, 0, n_cen)
+            consume(g * n_cen, g, 0, n_cen, owner=owner)
             return
 
         def one(ci, _):
-            consume(g * n_cen + ci, g, ci)
+            consume(g * n_cen + ci, g, ci, owner=owner)
             return 0
 
         lax.fori_loop(0, n_cen, one, 0)
@@ -345,46 +355,55 @@
         if i > 0:
             norm_arrived(zi, x)
             for j in range(1, n_cen):
-                rest_of(block(zi, x, c_at(j)), HALF, c_rest.at[seat(zi, j)])
+                b = block(zi, x, c_at(j))
+                for q in range(HALF):
+                    if by_line(q):
+                        arrived(allc.at[b, rows_of(q)], c_slot(zi, j, q))
+                rest_of(b, HALF, c_rest.at[seat(zi, j)])
 
     def x_ready(i):
         zi = ordered(i)
         norm_arrived(zi, 1 - x)
-        rest_of(block(zi, 1 - x, c), 0, x_rest.at[zi])
+        b = block(zi, 1 - x, c)
+        rest_of(b, 0, x_rest.at[zi])
+        if i > 0:
+            for q in range(HALF, PIECES):
+                if by_line(q):
+                    arrived(allc.at[b, rows_of(q)], x_slot(zi, q))
 
     def cross_ready(i):
         x_ready(i)
         for j in range(1, n_cen):
             corner_ready(ordered(i), j)
 
-    def take_line(i):
-        consume_group(ordered(i) * 2 + x)
-
-    def take_cross(i):
-        consume_group(ordered(i) * 2 + 1 - x)
-
-    def take_last_b(i):
+    def take_line(i, owner=None):
+        consume_group(ordered(i) * 2 + x, owner)
+
+    def take_cross(i, owner=None):
+        consume_group(ordered(i) * 2 + 1 - x, owner)
+
+    def take_last_b(i, owner):
         zi = ordered(i)
-        consume(block(zi, 1 - x, c), zi * 2 + 1 - x, c)
+        consume(block(zi, 1 - x, c), zi * 2 + 1 - x, c, owner=owner)
 
     def take_last_d(i, owner):
         zi = ordered(i)
         for j in range(1, n_cen):
             consume(block(zi, 1 - x, c_at(j)), zi * 2 + 1 - x, c_at(j), owner=owner)
 
-    def cross_stats(j, first):
+    def cross_stats(j):
         b = block(z, x, c_at(j))
 
         def step(i, carry):
-            return stats_step(allc[b, pl.ds(first, n // 2), :], i, carry)
-
-        running = fresh(n // 2)
+            return stats_step(allc[b], i, carry)
+
+        running = fresh(n)
         if n_cen <= 2:
             for i in range(tiles):
                 running = step(i, running)
         else:
             running = lax.fori_loop(0, tiles, step, running)
-        keep_stats(j, first, running)
+        keep_stats(j, running)
 
     def share_stats():
         for j in range(1, n_cen):
@@ -417,27 +436,30 @@
         )
 
     total_steps = n_z * PIECES
-    norm_at, early_at = 2 * PIECES - 1, (n_z - 1) * PIECES - 1
+    norm_at = 2 * PIECES - 1
 
     diagonals = {}
-    for q in range(PIECES):
-        diagonals.setdefault(min(PIECES + 1 + (q + 1) // 2, total_steps - 1), []).append((0, q))
+    for q, s in enumerate((1, 3, 2, 3)):
+        diagonals.setdefault(min(PIECES + s, total_steps - 1), []).append((0, q))
     for d in range(1, n_z):
         for e in range(2):
-            s = min(PIECES + 2 + 3 * d + e, total_steps - 1)
-            diagonals.setdefault(s, []).append((d, HALF - 1 + e))
+            s = min(2 * PIECES + 1 + 3 * (d - 1) + e, total_steps - 1)
+            diagonals.setdefault(s, []).append((d, LINE_PIECES[e]))
     for s in range(total_steps):
         i, q = 1 + s // PIECES, s % PIECES
         with jax.named_scope(f"move{s}"):
             if i < n_z:
                 if i == 1:
-                    line_forward(1, q)
-                line_step(i, q)
-                aside(ordered(i), q)
+                    line_forward(1, ORDER[q])
+                line_step(i, ORDER[q])
+                if i == 1:
+                    cross_step(0, q)
+                aside(ordered(i), ORDER[q])
                 if i > 1 and q < 2:
-                    for ahead in range(PIECES - 1) if q == 0 else (PIECES - 1,):
+                    for ahead in ORDER[:-1] if q == 0 else ORDER[-1:]:
                         line_forward(i, ahead)
-            cross_step(i - 1, q)
+            if i > 1 and q % 2 == 0:
+                cross_step(i - 1, q + 1)
             for d, piece_index in diagonals.get(s, ()):
                 diagonal_step(d, piece_index)
             if s <= max(n_z - 2, 2 * (n_z - 2)):
@@ -445,61 +467,33 @@
         with jax.named_scope(f"work{s}"):
             if s == PIECES - 1:
                 for j in range(1, n_cen):
-                    cross_stats(j, 0)
                     rest_of(block(z, x, c_at(j)), HALF, c_rest.at[seat(z, j)])
-                    cross_stats(j, n // 2)
+                    cross_stats(j)
                 share_stats()
             if s == norm_at:
                 share_norm()
                 take_line(0)
-            if s == early_at:
-                line_ready(1)
-                take_line(1)
+    last = n_z - 1
+    takes = []
+    for i in range(1, n_z):
+        takes += [
+            (functools.partial(line_ready, i), functools.partial(take_line, i)),
+            (functools.partial(cross_ready, i - 1), functools.partial(take_cross, i - 1)),
+        ]
+    takes.append((functools.partial(x_ready, last), functools.partial(take_last_b, last)))
+    ahead = 2
     with jax.named_scope("tail"):
-        last = n_z - 1
-        cross_ready(0)
-        for i in range(2, n_z):
-            line_ready(i)
-            if i < last:
-                cross_ready(i - 1)
-                take_cross(i - 2)
-                take_line(i)
-        cross_ready(last - 1)
-        x_ready(last)
-        take_cross(last - 2)
-        take_line(last)
-        take_cross(last - 1)
-        take_last_b(last)
-    with jax.named_scope("tail_d"):
-        for j in range(1, n_cen):
-            corner_ready(ordered(last), j)
-        take_last_d(last, 1 - core)
-
-    with jax.named_scope("pair"):
-        sums = remote(
-            weighted.at[1 - core], other_sums, send_pair.at[0], pair_sem.at[0], core_peer
-        )
-        tally = remote(
-            counts.at[1 - core], other_counts, send_pair.at[1], pair_sem.at[1], core_peer
-        )
-        tally.start()
-        sums.start()
-        take_last_d(last, core)
-        own_rows = pl.ds(pl.multiple_of(p * n_own, n_own), n_own)
-        tally.wait()
-        share = 1.0 / (
-            jnp.sum(counts[core] + other_counts[...], axis=1, keepdims=True) + 1.0
-        )
-        sums.wait()
-    with jax.named_scope("final"):
-        out_ref[...] = (
-            weighted[core] + other_sums[...] + cen_ref[own_rows, :].astype(jnp.float32)
-        ) * share
-
+        for first in range(0, len(takes), 2):
+            for ready, _ in takes[first:first + 2]:
+                ready()
+            for _, take in takes[first:first + 2]:
+                take(owner=1 - core)
+        for _, take in takes[:ahead]:
+            take(owner=core)
     with jax.named_scope("sent"):
 
         def left(ref, send_sem):
-            remote(ref, ref, send_sem, pair_sem.at[0], core_peer).wait_send()
+            remote(ref, ref, send_sem, line_sem.at[z, 0], core_peer).wait_send()
 
         left(allc.at[pl.ds(0, n_z)], send_x)
         left(allc.at[pl.ds(0, others * n_z)], send_c)
@@ -524,6 +518,34 @@
             )
         left(stat.at[pl.ds(0, others)], send_stat)
         left(norm.at[pl.ds(0, 2 * n_z - 1)], send_norm)
+
+    with jax.named_scope("tail_d"):
+        for j in range(1, n_cen):
+            corner_ready(ordered(last), j)
+        take_last_d(last, 1 - core)
+
+    with jax.named_scope("pair"):
+        sums = remote(
+            weighted.at[1 - core], other_sums, send_x, line_sem.at[z, 0], core_peer
+        )
+        tally = remote(
+            counts.at[1 - core], other_counts, send_c, line_sem.at[z, 1], core_peer
+        )
+        tally.start()
+        sums.start()
+        for _, take in takes[ahead:]:
+            take(owner=core)
+        take_last_d(last, core)
+        own_rows = pl.ds(pl.multiple_of(p * n_own, n_own), n_own)
+        tally.wait()
+        share = 1.0 / (
+            jnp.sum(counts[core] + other_counts[...], axis=1, keepdims=True) + 1.0
+        )
+        sums.wait()
+    with jax.named_scope("final"):
+        out_ref[...] = (
+            weighted[core] + other_sums[...] + cen_ref[own_rows, :].astype(jnp.float32)
+        ) * share
 
 
 def finish(fresh_ref, pen_ref, out_ref, cost_ref):
@@ -553,7 +575,6 @@
             vmem(first_bias.shape, first_bias.dtype),
             vmem(second_weight.shape, second_weight.dtype),
             vmem(centroids.shape[1:], centroids.dtype),
-            dma((5,)),
             vmem((2 * n_z * n_cen, n, width), jnp.bfloat16),
             vmem((n_cen, 1, 2 * n_cen * n), f32),
             vmem((2 * n_z, 1, n_cen * n), f32),
@@ -570,9 +591,7 @@
             dma((n_z * others, PIECES)),
             dma((others,)),
             dma((2 * n_z,)),
-            dma((2,)),
             *([dma] * 10),
-            dma((2,)),
             pltpu.SemaphoreType.REGULAR((3,)),
         ],
         compiler_params=pltpu.CompilerParams(

time: 27.3 us -> 27 us (0.989)
  Pallas kernels: 26.5 us -> 26.2 us
where the time goes in v4:
time: 27 us; the launch traced here: 26.9 us
  Pallas kernels  26.2 us (97%)
  between operations  0.64 us (2%)
    pallas_call x1, Pallas kernels, body(): pl.pallas_call(functools.partial(kernel, n_pts, n_cen), out_shape=(vmem((...  25.5 us
    pallas_call x1, Pallas kernels, body(): pl.pallas_call(finish, out_shape=(jax.ShapeDtypeStruct((1, owned, width),...  0.72 us

profile of v4, /device:TPU:0, one launch (start us, length us, event | category | flops | bytes accessed | tf_op | source)
XLA Modules:
  0.0 26.9 jit_solution(6537042940319992659)
XLA Ops:
  0.6 25.5 %shard_map.68 = (f32[256,256]{1,0:T(8,128)S(1)}, f32[1,256]{1,0:T(1,128)S(1)}) custom-call(bf16[256,512]{1,0:T(8,128)(2,1)} %states_hbm.1, bf16[512,1024]{1,0:T(8,128)(2,1)} %first_hbm.1, f32[1024]{0:T(1024)} %bias_hbm.1, bf16[1024,256]{1,0:T(8,128)(2,1)} %second_hbm.1, bf16[1,4096,256]{2,1,0:T(8,128)(2,1)} %cen_hbm.1), custom_call_target="tpu_custom_call" | custom-call | tf_op jit(solution)/shard_map/pallas_call | solution.py:567
  26.2 0.7 %shard_map.69 = (f32[1,256,256]{2,1,0:T(8,128)}, f32[256]{0:T(256)}) custom-call(f32[256,256]{1,0:T(8,128)S(1)} %get-tuple-element.4.fresh_ref, f32[1,256]{1,0:T(1,128)S(1)} %get-tuple-element.5.pen_ref), custom_call_target="tpu_custom_call" | custom-call | tf_op jit(solution)/shard_map/pallas_call | solution.py:601

commit v5 on v4

--- a/solution.py
+++ b/solution.py
@@ -140,6 +140,17 @@
     def line_arrived(zi, q):
         arrived(allc.at[block(zi, x, c), rows_of(q)], line_sem.at[zi, q])
 
+    def straight(i, q):
+        zi = ordered(i)
+        b = block(zi, x, c)
+        for j in range(1, n_cen):
+            pl.when(jnp.abs(zi - z) > 1)(
+                functools.partial(
+                    send, b, q, send_dx if q < HALF else send_dc,
+                    d_slot(zi, n_cen - j, q), at(z, 1 - x, c_at(j)),
+                )
+            )
+
     def line_forward(d, q):
         def visit(zi):
             @pl.when(passes(zi))
@@ -187,12 +198,22 @@
                     functools.partial(send, b, q, send_dc, d_slot(zi, n_cen - j, q), c_peer(j))
                 )
 
+    def last_of(at_z):
+        return jnp.where(at_z <= n_z - 1 - at_z, n_z - 1, 0)
+
+    def onward(zi, q):
+        up, down = passes_up(zi), passes_down(zi)
+        if q != LINE_PIECES[0] and n_z > 2:
+            up = jnp.logical_and(up, zi != last_of(z + 1))
+            down = jnp.logical_and(down, zi != last_of(z - 1))
+        return up, down
+
     def diagonal_step(d, q):
         def visit(zi):
             for j in range(1, n_cen):
                 b = block(zi, 1 - x, c_at(j))
                 slot = d_slot(zi, j, q)
-                up, down = passes_up(zi), passes_down(zi)
+                up, down = onward(zi, q)
                 pl.when(jnp.logical_or(up, down))(
                     functools.partial(arrived, allc.at[b, rows_of(q)], slot)
                 )
@@ -204,7 +225,7 @@
     def corner_ready(zi, j):
         b = block(zi, 1 - x, c_at(j))
         for q in range(PIECES):
-            seen = passes(zi) if by_line(q) else zi == z
+            seen = jnp.logical_or(*onward(zi, q)) if by_line(q) else zi == z
             pl.when(jnp.logical_not(seen))(
                 functools.partial(arrived, allc.at[b, rows_of(q)], d_slot(zi, j, q))
             )
@@ -357,7 +378,7 @@
             for j in range(1, n_cen):
                 b = block(zi, x, c_at(j))
                 for q in range(HALF):
-                    if by_line(q):
+                    if by_line(q) or i == n_z - 1:
                         arrived(allc.at[b, rows_of(q)], c_slot(zi, j, q))
                 rest_of(b, HALF, c_rest.at[seat(zi, j)])
 
@@ -368,7 +389,7 @@
         rest_of(b, 0, x_rest.at[zi])
         if i > 0:
             for q in range(HALF, PIECES):
-                if by_line(q):
+                if by_line(q) or i == n_z - 1:
                     arrived(allc.at[b, rows_of(q)], x_slot(zi, q))
 
     def cross_ready(i):
@@ -454,11 +475,13 @@
                 line_step(i, ORDER[q])
                 if i == 1:
                     cross_step(0, q)
+                if i == n_z - 1 and ORDER[q] != LINE_PIECES[0]:
+                    straight(i, ORDER[q])
                 aside(ordered(i), ORDER[q])
                 if i > 1 and q < 2:
                     for ahead in ORDER[:-1] if q == 0 else ORDER[-1:]:
                         line_forward(i, ahead)
-            if i > 1 and q % 2 == 0:
+            if 1 < i < n_z and q % 2 == 0:
                 cross_step(i - 1, q + 1)
             for d, piece_index in diagonals.get(s, ()):
                 diagonal_step(d, piece_index)
@@ -481,15 +504,12 @@
             (functools.partial(cross_ready, i - 1), functools.partial(take_cross, i - 1)),
         ]
     takes.append((functools.partial(x_ready, last), functools.partial(take_last_b, last)))
-    ahead = 2
+    split = len(takes) - 3
     with jax.named_scope("tail"):
-        for first in range(0, len(takes), 2):
-            for ready, _ in takes[first:first + 2]:
-                ready()
-            for _, take in takes[first:first + 2]:
-                take(owner=1 - core)
-        for _, take in takes[:ahead]:
-            take(owner=core)
+        for k, (ready, take) in enumerate(takes):
+            ready()
+            take(owner=None if k < split else 1 - core)
+
     with jax.named_scope("sent"):
 
         def left(ref, send_sem):
@@ -500,8 +520,9 @@
 
         def left_corner(near):
             corner = others * (HALF + (n_z - 1 - near) * (HALF - 1))
+            extra = others if n_z > 2 else 0
             left(allc.at[pl.ds(0, corner), rows_of(0)], send_dx)
-            left(allc.at[pl.ds(0, corner), rows_of(0)], send_dc)
+            left(allc.at[pl.ds(0, corner + extra), rows_of(0)], send_dc)
 
         inside = jnp.logical_and(has_up, has_down)
         pl.when(inside)(lambda: left_corner(2))
@@ -509,7 +530,8 @@
 
         def left_line(count, whole, parts):
             left(allc.at[pl.ds(0, count)], whole)
-            left(allc.at[pl.ds(0, (count + 1) * others), rows_of(0, 2)], parts)
+            pieces = others * (2 * (count + 1) - (1 if 2 * count >= n_z > 2 else 0))
+            left(allc.at[pl.ds(0, pieces), rows_of(0)], parts)
 
         for zi in range(n_z - 1):
             pl.when(z == zi)(functools.partial(left_line, zi + 1, send_up, send_dup))
@@ -533,7 +555,7 @@
         )
         tally.start()
         sums.start()
-        for _, take in takes[ahead:]:
+        for _, take in takes[split:]:
             take(owner=core)
         take_last_d(last, core)
         own_rows = pl.ds(pl.multiple_of(p * n_own, n_own), n_own)

time: 27 us -> 26.6 us (0.985)
  Pallas kernels: 26.2 us -> 25.8 us
    pallas_call x1, Pallas kernels: 25.5 us -> 25.1 us  [body(): pl.pallas_call(functools.partial(kernel, n_pts, n_cen), out_shape=(vmem((...]
where the time goes in v5:
time: 26.6 us; the launch traced here: 26.5 us
  Pallas kernels  25.8 us (97%)
  between operations  0.64 us (2%)
    pallas_call x1, Pallas kernels, body(): pl.pallas_call(functools.partial(kernel, n_pts, n_cen), out_shape=(vmem((...  25.1 us
    pallas_call x1, Pallas kernels, body(): pl.pallas_call(finish, out_shape=(jax.ShapeDtypeStruct((1, owned, width),...  0.72 us

profile of v5, /device:TPU:0, one launch (start us, length us, event | category | flops | bytes accessed | tf_op | source)
XLA Modules:
  0.0 26.5 jit_solution(1958776077929069371)
XLA Ops:
  0.6 25.1 %shard_map.68 = (f32[256,256]{1,0:T(8,128)S(1)}, f32[1,256]{1,0:T(1,128)S(1)}) custom-call(bf16[256,512]{1,0:T(8,128)(2,1)} %states_hbm.1, bf16[512,1024]{1,0:T(8,128)(2,1)} %first_hbm.1, f32[1024]{0:T(1024)} %bias_hbm.1, bf16[1024,256]{1,0:T(8,128)(2,1)} %second_hbm.1, bf16[1,4096,256]{2,1,0:T(8,128)(2,1)} %cen_hbm.1), custom_call_target="tpu_custom_call" | custom-call | tf_op jit(solution)/shard_map/pallas_call | solution.py:589
  25.7 0.7 %shard_map.69 = (f32[1,256,256]{2,1,0:T(8,128)}, f32[256]{0:T(256)}) custom-call(f32[256,256]{1,0:T(8,128)S(1)} %get-tuple-element.4.fresh_ref, f32[1,256]{1,0:T(1,128)S(1)} %get-tuple-element.5.pen_ref), custom_call_target="tpu_custom_call" | custom-call | tf_op jit(solution)/shard_map/pallas_call | solution.py:623

commit v6 on v5

--- a/solution.py
+++ b/solution.py
@@ -464,7 +464,7 @@
         diagonals.setdefault(min(PIECES + s, total_steps - 1), []).append((0, q))
     for d in range(1, n_z):
         for e in range(2):
-            s = min(2 * PIECES + 1 + 3 * (d - 1) + e, total_steps - 1)
+            s = min(2 * PIECES + 2 + 2 * (d - 1) + e, total_steps - 1)
             diagonals.setdefault(s, []).append((d, LINE_PIECES[e]))
     for s in range(total_steps):
         i, q = 1 + s // PIECES, s % PIECES

time: 26.6 us -> 26.6 us (level)
  no operation moved by 1% of the time
where the time goes in v6:
time: 26.6 us; the launch traced here: 26.5 us
  Pallas kernels  25.8 us (97%)
  between operations  0.64 us (2%)
    pallas_call x1, Pallas kernels, body(): pl.pallas_call(functools.partial(kernel, n_pts, n_cen), out_shape=(vmem((...  25.1 us
    pallas_call x1, Pallas kernels, body(): pl.pallas_call(finish, out_shape=(jax.ShapeDtypeStruct((1, owned, width),...  0.72 us

profile of v6, /device:TPU:0, one launch (start us, length us, event | category | flops | bytes accessed | tf_op | source)
XLA Modules:
  0.0 26.5 jit_solution(5142523368718716262)
XLA Ops:
  0.6 25.1 %shard_map.68 = (f32[256,256]{1,0:T(8,128)S(1)}, f32[1,256]{1,0:T(1,128)S(1)}) custom-call(bf16[256,512]{1,0:T(8,128)(2,1)} %states_hbm.1, bf16[512,1024]{1,0:T(8,128)(2,1)} %first_hbm.1, f32[1024]{0:T(1024)} %bias_hbm.1, bf16[1024,256]{1,0:T(8,128)(2,1)} %second_hbm.1, bf16[1,4096,256]{2,1,0:T(8,128)(2,1)} %cen_hbm.1), custom_call_target="tpu_custom_call" | custom-call | tf_op jit(solution)/shard_map/pallas_call | solution.py:589
  25.7 0.7 %shard_map.69 = (f32[1,256,256]{2,1,0:T(8,128)}, f32[256]{0:T(256)}) custom-call(f32[256,256]{1,0:T(8,128)S(1)} %get-tuple-element.4.fresh_ref, f32[1,256]{1,0:T(1,128)S(1)} %get-tuple-element.5.pen_ref), custom_call_target="tpu_custom_call" | custom-call | tf_op jit(solution)/shard_map/pallas_call | solution.py:623
